TPU v7x, 512 devices: a whole 4x4x16 slice. The times are simulated.
512 devices in a mesh: rows: 16 (over y, z_lo), cols: 32 (over z_hi, x, core).
Axes of the slice: x: 4, y: 4, z: 16 (z_hi: 4, z_lo: 4; z = z_hi * 4 + z_lo), core: 2. Of those that a mesh axis runs over, the one named last changes fastest.
Arguments:
- factor_u: float32 [16, 8192, 128], P('rows', 'cols'), may hold values from -2 to 2
- factor_v: float32 [32, 2048, 128], P('cols', 'rows'), may hold values from -2 to 2
- values: bfloat16 [16, 32, 32, 256, 256], P('rows', 'cols'), may hold values from -6 to 6
- mask_words: int32 [16, 32, 32, 16, 256], P('rows', 'cols'), may hold values from 0 to 65535, as said below
- tile_cols: int32 [16, 32, 32], P('rows', 'cols'), may hold values from 0 to 7
Outputs:
- new_u: float32 [16, 8192, 128], P('rows', 'cols')
- new_v: float32 [32, 2048, 128], P('cols', 'rows')
- loss: float32 [], replicated
Inputs may be any that keep to these rules, and one draw needn't show every extreme that they name: `mask_words`: bit b of word w of a slot marks the entry in row 16 w + b of the tile.
All inputs are finite; a program needn't handle non-finite values.
Results may differ from a plain program's by a relative error of at most 0.02.
Values may be sent and summed in bfloat16 or wider, within the bound.
A program may use at most 64 MiB of HBM per device.

v0:
```python
import jax
import jax.numpy as jnp
from jax import lax
from jax.sharding import Mesh
from jax.sharding import PartitionSpec as P

ROWS = ("rows_0", "rows_1")
COLS = ("cols_0", "cols_1", "cols_2")
ROWS_COLS = ("rows_0", "rows_1", "cols_0", "cols_1", "cols_2")


step_rate = 0.01
ridge_weight = 0.1


def from_everyone(array, axis):
    copies = jnp.broadcast_to(array, (lax.axis_size(axis), *array.shape))
    return lax.all_to_all(copies, axis, split_axis=0, concat_axis=0, tiled=True)


def laid_out(tiles, dim):
    tiles = jnp.moveaxis(tiles, 0, dim)
    dims = tiles.shape
    return tiles.reshape(*dims[:dim], dims[dim] * dims[dim + 1], *dims[dim + 2 :])


def gathered_copies(array, axis, dim):
    tiles = from_everyone(array, axis)
    return laid_out(tiles, dim)


def in_blocks(array, dim, count):
    dims = array.shape
    tiles = array.reshape(*dims[:dim], count, dims[dim] // count, *dims[dim + 1 :])
    return jnp.moveaxis(tiles, dim, 0)


def sum_by_chip(array, chips, core, dim):
    sizes = (lax.axis_size(chips), lax.axis_size(core))
    tiles = in_blocks(array, dim, sizes[0] * sizes[1])
    inside = tiles.shape[1:]
    tiles = tiles.reshape(*sizes, *inside).swapaxes(0, 1).reshape(-1, *inside)
    tiles = lax.psum_scatter(tiles, core, scatter_dimension=0, tiled=True)
    return lax.psum_scatter(tiles, chips, scatter_dimension=0, tiled=True)[0]


def summed_on_arrival(array, axis, dim):
    count = lax.axis_size(axis)
    tiles = lax.all_to_all(in_blocks(array, dim, count), axis, 0, 0, tiled=True)
    return jnp.sum(tiles.astype(jnp.float32), axis=0)


def by_axis(array, axes):
    for axis in axes:
        array = lax.psum(array, axis)
    return array


def decode(mask_bits):
    shifts = jnp.arange(16, dtype=jnp.int32)
    bit_values = jnp.bitwise_and(
        jnp.right_shift(mask_bits[:, :, None, :], shifts[None, None, :, None]), 1
    )
    return bit_values.reshape(
        mask_bits.shape[0], mask_bits.shape[1] * 16, mask_bits.shape[2]
    ).astype(jnp.float32)


def slot_terms(left_rows, tile_values, mask_bits, column_ids, right_tiles):
    observed = decode(mask_bits)
    right_rows = jnp.take(right_tiles, column_ids, axis=0)
    predicted = jnp.einsum(
        "sik,sjk->sij", left_rows, right_rows, preferred_element_type=jnp.float32
    )
    residual = observed * (predicted - tile_values.astype(jnp.float32))
    squares = 0.5 * jnp.sum(residual * residual)
    resid_low = residual.astype(jnp.bfloat16)
    grad_rows = jnp.einsum(
        "sij,sjk->sik", resid_low, right_rows, preferred_element_type=jnp.float32
    )
    first = grad_rows.reshape(-1, left_rows.shape[2])
    grad_cols = jnp.einsum("sij,sik->sjk", resid_low, left_rows, preferred_element_type=jnp.float32)
    selector = (
        column_ids[:, None] == jnp.arange(right_tiles.shape[0], dtype=jnp.int32)[None, :]
    ).astype(jnp.float32)
    col_sums = jnp.einsum(
        "sq,sx->qx",
        selector,
        grad_cols.reshape(grad_cols.shape[0], -1),
        precision=lax.Precision.HIGHEST,
        preferred_element_type=jnp.float32,
    )
    return (first, col_sums, squares)


def band_terms(left_tiles, tile_values, mask_bits, column_ids, right_tiles):
    tile_count = left_tiles.shape[0]
    row_parts = []
    col_total = jnp.zeros(
        (right_tiles.shape[0], right_tiles.shape[1] * right_tiles.shape[2]), jnp.float32
    )
    square_total = jnp.zeros((), jnp.float32)
    for block_start in range(0, tile_count, 8):
        block_len = min(8, tile_count - block_start)
        block_end = block_start + block_len
        first, col_sums, squares = slot_terms(
            left_tiles[block_start:block_end],
            tile_values[block_start:block_end],
            mask_bits[block_start:block_end],
            column_ids[block_start:block_end],
            right_tiles,
        )
        row_parts.append(first)
        col_total = col_total + col_sums
        square_total = square_total + squares
    return (jnp.concatenate(row_parts, axis=0), col_total, square_total)


def per_device(factor_u, factor_v, values, mask_words, tile_cols):
    owned_left = factor_u[0]
    owned_right = factor_v[0]
    tile_values = values[0, 0]
    mask_bits = mask_words[0, 0]
    column_ids = tile_cols[0, 0]
    tile_size = tile_values.shape[-1]
    factor_rank = owned_left.shape[-1]
    slot_count = tile_values.shape[0]
    v_band = gathered_copies(owned_right.astype(jnp.bfloat16), ROWS, 0)
    right_tiles = v_band.reshape(-1, tile_size, factor_rank)
    u_low = owned_left.astype(jnp.bfloat16)
    u_band = lax.all_gather(u_low, COLS, axis=0, tiled=True)
    first_rows, col_total, square_total = band_terms(
        u_band.reshape(-1, tile_size, factor_rank), tile_values, mask_bits, column_ids, right_tiles
    )
    grad_u = sum_by_chip(first_rows.astype(jnp.bfloat16), ("cols_0", "cols_1"), "cols_2", 0).astype(
        jnp.float32
    )
    grad_v = summed_on_arrival(col_total.reshape(-1, factor_rank).astype(jnp.bfloat16), ROWS, 0)
    local_sum = square_total + 0.5 * ridge_weight * (
        jnp.sum(owned_left * owned_left) + jnp.sum(owned_right * owned_right)
    )
    total = by_axis(local_sum, ROWS_COLS)
    entries = lax.axis_size(ROWS) * lax.axis_size(COLS) * slot_count * tile_size * tile_size
    new_left = owned_left - step_rate * (grad_u + ridge_weight * owned_left)
    new_right = owned_right - step_rate * (grad_v + ridge_weight * owned_right)
    return (new_left[None], new_right[None], total / entries)


def solution(mesh):
    split = Mesh(
        mesh.devices.reshape(4, 4, 4, 4, 2), ("rows_0", "rows_1", "cols_0", "cols_1", "cols_2")
    )
    in_specs = (
        P(ROWS, COLS, None),
        P(COLS, ROWS, None),
        P(ROWS, COLS, None, None, None),
        P(ROWS, COLS, None, None, None),
        P(ROWS, COLS, None),
    )
    out_specs = (P(ROWS, COLS, None), P(COLS, ROWS, None), P())
    return jax.shard_map(
        per_device, mesh=split, in_specs=in_specs, out_specs=out_specs, check_vma=False
    )
```

profile of v0, /device:TPU:1, one launch (start us, length us, event | category | flops | bytes accessed | tf_op | source)
XLA Modules:
  0.0 256.1 jit_solution(2091023990044940334)
XLA Ops:
  7.2 2.2 multiply_reduce_fusion.4
  9.5 1.5 multiply_reduce_fusion.5
  11.9 9.2 %all-to-all-start = ((bf16[16,128,128]{2,1,0:T(8,128)(2,1)}), bf16[16,128,128]{2,1,0:T(8,128)(2,1)S(1)}, u32[]{:S(2)}, u32[]{:S(2)}) async-start(bf16[16,128,128]{2,1,0:T(8,128)(2,1)} %broadcast_in_dim.11), calls=%async_computation | async-start | bytes 1048576 | tf_op jit(solution)/shard_map/all_to_all | solution.py:18
  21.1 3.9 %fusion.36 = (bf16[1,1,8,256,256]{4,3,2,1,0:T(8,128)(2,1)}, bf16[1,1,8,256,256]{4,3,2,1,0:T(8,128)(2,1)}, bf16[1,1,8,256,256]{4,3,2,1,0:T(8,128)(2,1)}, bf16[1,1,8,256,256]{4,3,2,1,0:T(8,128)(2,1)S(1)}) fusion(bf16[1,1,32,256,256]{4,3,2,1,0:T(8,128)(2,1)} %param.9), kind=kLoop, calls=%fused_computation.94 | loop fusion | bytes 8388608 | tf_op jit(solution)/shard_map/slice | solution.py:108
  26.4 1.5 shift_right_arithmetic.104
  27.9 1.9 copy.30
  29.9 2.2 copy.40
  32.2 1.6 shift_right_arithmetic.100
  33.7 2.9 %copy.27 = s32[8,256,256]{1,2,0:T(8,128)} copy(s32[8,256,256]{2,1,0:T(8,128)} %bitcast.116) | data formatting | bytes 4194304 | tf_op jit(solution)/shard_map/shift_right_arithmetic | solution.py:62
  36.7 2.3 copy.39
  38.9 1.5 shift_right_arithmetic.96
  40.4 2.9 %copy.24 = s32[8,256,256]{1,2,0:T(8,128)} copy(s32[8,256,256]{2,1,0:T(8,128)} %bitcast.117) | data formatting | bytes 4194304 | tf_op jit(solution)/shard_map/shift_right_arithmetic | solution.py:62
  43.3 2.3 copy.38
  45.6 1.5 shift_right_arithmetic.89
  47.1 2.9 %copy.21 = s32[8,256,256]{1,2,0:T(8,128)} copy(s32[8,256,256]{2,1,0:T(8,128)} %bitcast.118) | data formatting | bytes 4194304 | tf_op jit(solution)/shard_map/shift_right_arithmetic | solution.py:62
  54.3 1.4 gather_fusion
  55.8 40.2 %all-gather.3.cloned.1.call-done = bf16[1,8192,128]{2,1,0:T(8,128)(2,1)} async-done(((bf16[1,256,128]{2,1,0:T(8,128)(2,1)}), bf16[1,8192,128]{2,1,0:T(8,128)(2,1)}) %all-gather.3.cloned.1.call-update) | async-done | bytes 2097168 | tf_op jit(solution)/shard_map/all_gather | solution.py:131
  96.0 1.8 fusion.37
  98.6 1.5 multiply_reduce_fusion
  101.7 1.5 multiply_reduce_fusion.1
  104.7 1.5 multiply_reduce_fusion.2
  107.9 1.5 multiply_reduce_fusion.3
  111.0 1.6 copy.33
  112.7 1.8 convolution_bitcast_fusion.3
  122.1 4.3 %all-to-all-start.1 = ((bf16[16,128,128]{2,1,0:T(8,128)(2,1)}), bf16[16,128,128]{2,1,0:T(8,128)(2,1)S(1)}, u32[]{:S(2)}, u32[]{:S(2)}) async-start(bf16[16,128,128]{2,1,0:T(8,128)(2,1)} %convert_element_type.106), calls=%async_computation.3 | async-start | bytes 1048576 | tf_op jit(solution)/shard_map/all_to_all | solution.py:49
  131.6 8.7 %psum.35 = f32[]{:T(128)} all-reduce(f32[]{:T(128)S(6)} %add.61), channel_id=1, replica_groups=mesh['rows_0'=4,'rows_1'=4,'cols_0'=4,'cols_1'=4,'cols_2'=2] {'rows_0'}, use_global_device_ids=true, to_apply=%region_9.11 | all-reduce | flops 1 | bytes 8 | tf_op jit(solution)/shard_map/psum | solution.py:55
  140.4 10.4 %psum.36 = f32[]{:T(128)} all-reduce(f32[]{:T(128)} %psum.35), channel_id=1, replica_groups=mesh['rows_0'=4,'rows_1'=4,'cols_0'=4,'cols_1'=4,'cols_2'=2] {'rows_1'}, use_global_device_ids=true, to_apply=%region_10.12 | all-reduce | flops 1 | bytes 8 | tf_op jit(solution)/shard_map/psum | solution.py:55
  150.7 15.0 %psum.37 = f32[]{:T(128)} all-reduce(f32[]{:T(128)} %psum.36), channel_id=1, replica_groups=mesh['rows_0'=4,'rows_1'=4,'cols_0'=4,'cols_1'=4,'cols_2'=2] {'cols_0'}, use_global_device_ids=true, to_apply=%region_11.13 | all-reduce | flops 1 | bytes 8 | tf_op jit(solution)/shard_map/psum | solution.py:55
  165.8 9.9 %psum.38 = f32[]{:T(128)} all-reduce(f32[]{:T(128)} %psum.37), channel_id=1, replica_groups=mesh['rows_0'=4,'rows_1'=4,'cols_0'=4,'cols_1'=4,'cols_2'=2] {'cols_1'}, use_global_device_ids=true, to_apply=%region_12.14 | all-reduce | flops 1 | bytes 8 | tf_op jit(solution)/shard_map/psum | solution.py:55
  175.7 9.9 %psum.39 = f32[]{:T(128)} all-reduce(f32[]{:T(128)} %psum.38), channel_id=1, replica_groups=mesh['rows_0'=4,'rows_1'=4,'cols_0'=4,'cols_1'=4,'cols_2'=2] {'cols_2'}, use_global_device_ids=true, to_apply=%region_13.15 | all-reduce | flops 1 | bytes 8 | tf_op jit(solution)/shard_map/psum | solution.py:55
  186.9 59.9 %reduce-scatter.5.cloned.1.call-done = bf16[1,256,128]{2,1,0:T(8,128)(2,1)} async-done(((bf16[16,256,128]{2,1,0:T(8,128)(2,1)}), bf16[1,256,128]{2,1,0:T(8,128)(2,1)}) %reduce-scatter.5.cloned.1.call-update) | async-done | bytes 65552 | tf_op jit(solution)/shard_map/reduce_scatter | solution.py:44
  246.9 1.5 multiply_subtract_fusion
  (82 shorter events, 23.5 us)
Async XLA Ops:
  7.2 88.9 %all-gather.3.cloned.1.call-start = ((), (), s32[]{:S(2)}) async-start(), calls=%async_computation.6 | async-start | bytes 2162688 | tf_op jit(solution)/shard_map/all_gather | solution.py:131
  11.9 38.2 %all-to-all-start = ((bf16[16,128,128]{2,1,0:T(8,128)(2,1)}), bf16[16,128,128]{2,1,0:T(8,128)(2,1)S(1)}, u32[]{:S(2)}, u32[]{:S(2)}) async-start(bf16[16,128,128]{2,1,0:T(8,128)(2,1)} %broadcast_in_dim.11), calls=%async_computation | async-start | bytes 1048576 | tf_op jit(solution)/shard_map/all_to_all | solution.py:18
  21.1 106.7 %reduce-scatter.3.cloned.1.call-start = ((), (), s32[]{:S(2)}) async-start(), calls=%async_computation.4 | async-start | bytes 3145728 | tf_op jit(solution)/shard_map/reduce_scatter | solution.py:43
  25.0 1.3 copy-start.19
  47.1 2.9 %copy-start.22 = (s32[1,1,32]{2,1,0:T(1,128)S(1)}, s32[1,1,32]{2,1,0:T(1,128)}, u32[]{:S(2)}) copy-start(s32[1,1,32]{2,1,0:T(1,128)} %param.11) | copy-start | bytes 388
  96.0 2.6 %copy-start.7 = (bf16[8,256,128]{2,1,0:T(8,128)(2,1)S(1)}, bf16[8,256,128]{2,1,0:T(8,128)(2,1)}, u32[]{:S(2)}) copy-start(bf16[8,256,128]{2,1,0:T(8,128)(2,1)} %gather_fusion.3) | copy-start | bytes 1572868
  96.0 2.6 %copy-start.15 = (bf16[1,1,8,256,256]{3,4,2,1,0:T(8,128)(2,1)S(1)}, bf16[1,1,8,256,256]{3,4,2,1,0:T(8,128)(2,1)}, u32[]{:S(2)}) copy-start(bf16[1,1,8,256,256]{3,4,2,1,0:T(8,128)(2,1)} %copy.41) | copy-start | bytes 3145732
  97.8 0.8 copy-start.8
  97.8 2.8 %copy-start.10 = (bf16[1,2048,128]{2,1,0:T(8,128)(2,1)}, bf16[1,2048,128]{2,1,0:T(8,128)(2,1)S(1)}, u32[]{:S(2)}) copy-start(bf16[1,2048,128]{2,1,0:T(8,128)(2,1)S(1)} %get-tuple-element.17) | copy-start | bytes 1572868
  97.8 5.9 %copy-start.12 = (bf16[1,2048,128]{2,1,0:T(8,128)(2,1)}, bf16[1,2048,128]{2,1,0:T(8,128)(2,1)S(1)}, u32[]{:S(2)}) copy-start(bf16[1,2048,128]{2,1,0:T(8,128)(2,1)S(1)} %get-tuple-element.18) | copy-start | bytes 1572868
  97.8 9.0 %copy-start.14 = (bf16[1,2048,128]{2,1,0:T(8,128)(2,1)}, bf16[1,2048,128]{2,1,0:T(8,128)(2,1)S(1)}, u32[]{:S(2)}) copy-start(bf16[1,2048,128]{2,1,0:T(8,128)(2,1)S(1)} %get-tuple-element.16) | copy-start | bytes 1572868
  98.6 2.0 copy-start.6
  98.6 2.0 copy-start.18
  100.1 1.6 copy-start.3
  101.7 2.0 copy-start.5
  101.7 2.0 copy-start.17
  103.1 1.6 copy-start.2
  104.7 2.1 copy-start.4
  104.7 2.1 copy-start.16
  106.3 1.6 copy-start.1
  109.4 1.0 copy-start
  112.6 1.9 copy-start.13
  112.7 2.3 copy-start.11
  114.6 1.0 copy-start.9
  121.0 65.3 %copy-start.21 = (f32[1,128,128]{2,1,0:T(8,128)S(1)}, f32[1,128,128]{2,1,0:T(8,128)}, u32[]{:S(2)}) copy-start(f32[1,128,128]{2,1,0:T(8,128)} %param.8) | copy-start | bytes 196612
  121.1 125.8 %copy-start.20 = (f32[1,256,128]{2,1,0:T(8,128)S(1)}, f32[1,256,128]{2,1,0:T(8,128)}, u32[]{:S(2)}) copy-start(f32[1,256,128]{2,1,0:T(8,128)} %param.7) | copy-start | bytes 393220
  122.1 64.1 %all-to-all-start.1 = ((bf16[16,128,128]{2,1,0:T(8,128)(2,1)}), bf16[16,128,128]{2,1,0:T(8,128)(2,1)S(1)}, u32[]{:S(2)}, u32[]{:S(2)}) async-start(bf16[16,128,128]{2,1,0:T(8,128)(2,1)} %convert_element_type.106), calls=%async_computation.3 | async-start | bytes 1048576 | tf_op jit(solution)/shard_map/all_to_all | solution.py:49
  126.5 120.4 %reduce-scatter.5.cloned.1.call-start = ((), (), s32[]{:S(2)}) async-start(), calls=%async_computation.5 | async-start | bytes 1114112 | tf_op jit(solution)/shard_map/reduce_scatter | solution.py:44
Sparse Core Ops, SparseCore 0:
  11.7 84.2 all-gather.2
  112.7 15.0 reduce-scatter.2
  131.9 114.9 reduce-scatter.4
where the time goes:
time: 257 us; the launch traced here: 256 us
  waiting for transfers between devices  102 us (40%)
  blocking collectives  53.9 us (21%)
  local copies, waits for them, and re-layouts  45 us (18%)
  between operations  19.7 us (8%)
  matrix products  16.1 us (6%)
  starting transfers between devices  13.6 us (5%)
  other arithmetic  6.22 us (2%)
    reduce_scatter x1, waiting for transfers between devices, sum_by_chip(): return lax.psum_scatter(tiles, chips, scatter_dimension=0, tiled=True)[0]  59.9 us
    psum x5, blocking collectives, by_axis(): array = lax.psum(array, axis)  53.9 us
    all_gather x1, waiting for transfers between devices, per_device(): u_band = lax.all_gather(u_low, COLS, axis=0, tiled=True)  40.2 us
    shift_right_arithmetic x11, local copies, waits for them, and re-layouts, decode(): jnp.right_shift(mask_bits[:, :, None, :], shifts[None, None, :, None])  16.8 us
    unnamed x50, local copies, waits for them, and re-layouts  13.2 us
    all_to_all x1, starting transfers between devices, from_everyone(): return lax.all_to_all(copies, axis, split_axis=0, concat_axis=0, tiled=True)  9.17 us
    dot_general x4, matrix products, slot_terms(): jnp.einsum('sik,sjk->sij', left_rows, right_rows, preferred_element_type=...  5.97 us
    gather x4, local copies, waits for them, and re-layouts, slot_terms(): right_rows = jnp.take(right_tiles, column_ids, axis=0)  5.66 us
  transfers between devices with their start and end apart: 5, of which 3 were waited for; matrix products, arithmetic and copies ran while one was open for 18% of the time, Pallas kernels for 0%

commit v1 on v0

v1 whole, which is shorter than its diff:
```python
import jax
import jax.numpy as jnp
from jax import lax
from jax.experimental import pallas as pl
from jax.experimental.pallas import tpu as pltpu
from jax.sharding import PartitionSpec as P

F32 = jnp.float32
BF16 = jnp.bfloat16
STEP = 0.01
RIDGE = 0.1
MESH = pl.DeviceIdType.MESH
GROUP = 4


def wrap(i, n=4):
    return lax.rem(i + n, n)


class Place:
    def __init__(self):
        c = lax.axis_index("cols")
        r = lax.axis_index("rows")
        self.c, self.r = c, r
        self.k = lax.rem(c, 2)
        self.x = lax.rem(lax.div(c, 2), 4)
        self.zh = lax.div(c, 8)
        self.y = lax.div(r, 4)
        self.zl = lax.rem(r, 4)

    def col(self, dz=0, dx=0, dk=0):
        return wrap(self.zh + dz) * 8 + wrap(self.x + dx) * 2 + lax.rem(self.k + dk, 2)

    def row(self, dy=0, dl=0):
        return wrap(self.y + dy) * 4 + wrap(self.zl + dl)

    def dev(self, dz=0, dx=0, dk=0, dy=0, dl=0):
        if dy or dl:
            return {"rows": self.row(dy, dl)}
        return {"cols": self.col(dz, dx, dk)}


class Net:
    def __init__(self, send_sems, recv_sems):
        self.send_sems, self.recv_sems = send_sems, recv_sems
        self.ids, self.sent = {}, []

    def at(self, name):
        return self.ids.setdefault(name, len(self.ids))

    def send(self, name, src, dst, dev):
        i = self.at(name)
        copy = pltpu.make_async_remote_copy(
            src_ref=src, dst_ref=dst, send_sem=self.send_sems.at[i], recv_sem=self.recv_sems.at[i],
            device_id=dev, device_id_type=MESH)
        copy.start()
        self.sent.append(copy)

    def recv(self, name, ref, dev):
        i = self.at(name)
        pltpu.make_async_remote_copy(
            src_ref=ref, dst_ref=ref, send_sem=self.send_sems.at[i], recv_sem=self.recv_sems.at[i],
            device_id=dev, device_id_type=MESH).wait_recv()

    def finish(self):
        for copy in self.sent:
            copy.wait_send()


def greet(devs):
    barrier = pltpu.get_barrier_semaphore()
    for dev in devs:
        pl.semaphore_signal(barrier, inc=1, device_id=dev, device_id_type=MESH)
    pl.semaphore_wait(barrier, len(devs))


DZ = (0, -1, 1, 2)
N_GATHER = 80
N_REDUCE = 104


def gather_kernel(fu_ref, fv_ref, u_ref, v_ref, ridge_ref, send_sems, recv_sems):
    p = Place()
    net = Net(send_sems, recv_sems)
    u_ref[p.c] = fu_ref[...].astype(BF16)
    v_ref[p.r] = fv_ref[...].astype(BF16)
    greet([p.dev(dz=1), p.dev(dz=-1), p.dev(dx=1), p.dev(dx=-1), p.dev(dk=1),
           p.dev(dy=1), p.dev(dy=-1), p.dev(dl=1), p.dev(dl=2), p.dev(dl=3)])

    def ub(j, dx, h):
        return u_ref.at[p.col(DZ[j] if isinstance(j, int) else j[0], dx), pl.ds(h * 128, 128)]

    def vb(d, dy, h):
        return v_ref.at[p.row(dy, d), pl.ds(h * 64, 64)]

    class Ring:
        def __init__(self, tag, view, dev):
            self.tag, self.view, self.dev = tag, view, dev

        def put(self, j, h):
            for s in ((1, -1) if h == 0 else (-1, 1)):
                ref = self.view(j, 0, h)
                net.send((self.tag, j, s, h), ref, ref, self.dev(s))

        def forward(self, j):
            for s, h in ((1, 0), (-1, 1)):
                ref = self.view(j, -s, h)
                net.recv((self.tag, j, s, h), ref, self.dev(s))
                net.send((self.tag, j, s, "far"), ref, ref, self.dev(s))

        def finish(self, j, near=None, far=None):
            for s, h in ((1, 1), (-1, 0)):
                net.recv((self.tag, j, s, h), self.view(j, -s, h), self.dev(s))
            if near:
                near()
            for s, h in ((1, 0), (-1, 1)):
                net.recv((self.tag, j, s, "far"), self.view(j, 2, h), self.dev(s))
            if far:
                far()

    xr = Ring("x", ub, lambda s: p.dev(dx=s))
    yr = Ring("y", vb, lambda s: p.dev(dy=s))

    def twin(j, dx):
        ref = u_ref.at[p.col(DZ[j], dx)]
        net.send(("p", j, dx), ref, ref, p.dev(dk=1))

    def xfin(j):
        xr.finish(j, lambda: (twin(j, -1), twin(j, 1)), lambda: twin(j, 2))

    for s, h in ((1, 0), (-1, 1), (1, 1), (-1, 0)):
        ref = ub(0, 0, h)
        net.send(("z", s, h), ref, ref, p.dev(dz=s))
    for d in (1, 2, 3):
        ref = v_ref.at[p.r]
        net.send(("l", d), ref, ref, p.dev(dl=d))
    for h in (0, 1):
        xr.put(0, h)
    for h in (0, 1):
        yr.put(0, h)
    twin(0, 0)
    fu = fu_ref[...]
    fv = fv_ref[...]
    ridge_ref[...] = (0.5 * RIDGE) * (
        jnp.sum((fu * fu).reshape(32, 8, 128), axis=0) + jnp.sum((fv * fv).reshape(16, 8, 128), axis=0))
    xr.forward(0)
    yr.forward(0)
    for d in (1, 2, 3):
        net.recv(("l", d), v_ref.at[p.row(0, -d)], p.dev(dl=d))
        for h in (0, 1):
            yr.put(-d, h)
    xfin(0)

    def z_in(s, h, j):
        ref = ub(j, 0, h)
        net.recv(("z", s, h), ref, p.dev(dz=s))
        if (s, h) in ((1, 0), (-1, 1)):
            net.send(("z", s, "far"), ref, ref, p.dev(dz=s))
        xr.put(j, h)

    z_in(1, 0, 1)
    z_in(-1, 1, 2)
    for d in (1, 2, 3):
        yr.forward(-d)
    z_in(1, 1, 1)
    z_in(-1, 0, 2)
    twin(1, 0)
    twin(2, 0)
    xr.forward(1)
    xr.forward(2)
    for s, h in ((1, 0), (-1, 1)):
        net.recv(("z", s, "far"), ub(3, 0, h), p.dev(dz=s))
        xr.put(3, h)
    twin(3, 0)
    xfin(1)
    xfin(2)
    yr.finish(0)
    for d in (1, 2, 3):
        yr.finish(-d)
    xr.forward(3)
    xfin(3)
    for j in range(4):
        for dx in (0, -1, 1, 2):
            net.recv(("p", j, dx), u_ref.at[p.col(DZ[j], dx, 1)], p.dev(dk=1))
    net.finish()


def compute_kernel(ids_ref, u_ref, v_ref, vals_ref, mask_ref, ridge_ref, pu_ref, pv_ref, ls_ref, acc_v, acc_l):
    g = pl.program_id(0)

    @pl.when(g == 0)
    def _():
        acc_v[...] = jnp.zeros_like(acc_v)
        acc_l[...] = jnp.zeros_like(acc_l)

    probe = jnp.left_shift(1, lax.rem(lax.broadcasted_iota(jnp.int32, (16, 256), 0), 16))
    for i in range(GROUP):
        s = g * GROUP + i
        q = ids_ref[s]
        ut = u_ref[s]
        vt = v_ref[q]
        pred = lax.dot_general(ut, vt, (((1,), (1,)), ((), ())), preferred_element_type=F32)
        bits = jnp.concatenate(
            [jnp.bitwise_and(jnp.broadcast_to(mask_ref[i, w:w + 1, :], (16, 256)), probe) for w in range(16)], axis=0)
        res = jnp.where(bits != 0, pred - vals_ref[i].astype(F32), 0.0)
        acc_l[...] += jnp.sum((res * res).reshape(32, 8, 256), axis=0)
        low = res.astype(BF16)
        gu = jnp.dot(low, vt, preferred_element_type=F32)
        pu_ref[i % 2, 0, i // 2] = gu.astype(BF16)
        acc_v[q] += lax.dot_general(ut, low, (((0,), (0,)), ((), ())), preferred_element_type=F32)

    @pl.when(g == pl.num_programs(0) - 1)
    def _():
        for q in range(8):
            pv_ref[q] = acc_v[q].T.astype(BF16)
        half = acc_l[...]
        ls_ref[...] = 0.5 * (half[:, :128] + half[:, 128:]) + ridge_ref[...]


def reduce_kernel(entries, pu_ref, pv_ref, ls_ref, fu_ref, fv_ref, nu_ref, nv_ref, loss_ref,
                  pb, t, xb, xs, w, w0, zb, zs, yb, ys, wl, wl0, lb, le, ln, send_sems, recv_sems):
    p = Place()
    net = Net(send_sems, recv_sems)
    greet([p.dev(dk=1)] + [p.dev(dx=d) for d in (1, 2, 3)] + [p.dev(dz=d) for d in (1, 2, 3)]
          + [p.dev(dy=d) for d in (1, 2, 3)] + [p.dev(dl=d) for d in (1, 2, 3)])

    order = (3, 1, 2, 0)
    net.send(("lp",), ls_ref, le.at[0], p.dev(dk=1))
    for j in order:
        net.send(("p", j), pu_ref.at[1 - p.k, wrap(p.zh + DZ[j])], pb.at[j], p.dev(dk=1))

    def f(ref):
        return ref[...].astype(F32)

    class Ring:
        def __init__(self, tag, block, buf, mid, dev, half):
            self.tag, self.block, self.buf, self.mid, self.dev, self.half = tag, block, buf, mid, dev, half

        def part(self, j, i, h):
            return self.block(j, i).at[pl.ds(h * self.half, self.half)]

        def open(self, j):
            for s, h in ((1, 0), (-1, 1)):
                net.send((self.tag, j, s, "far"), self.part(j, 2, h), self.buf.at[j, h], self.dev(s))
            for s, h in ((1, 1), (-1, 0)):
                net.send((self.tag, j, s, "near"), self.part(j, s, h), self.buf.at[j, 2 + h], self.dev(s))

        def middle(self, j):
            for s, h in ((1, 0), (-1, 1)):
                net.recv((self.tag, j, s, "far"), self.buf.at[j, h], self.dev(s))
                self.mid[j, h] = (f(self.part(j, s, h)) + f(self.buf.at[j, h])).astype(BF16)
                net.send((self.tag, j, s, "mid"), self.mid.at[j, h], self.buf.at[j, 4 + h], self.dev(s))

        def close(self, j):
            out = []
            for s, h in ((1, 1), (-1, 0)):
                net.recv((self.tag, j, s, "near"), self.buf.at[j, 2 + h], self.dev(s))
            for s, h in ((1, 0), (-1, 1)):
                net.recv((self.tag, j, s, "mid"), self.buf.at[j, 4 + h], self.dev(s))
            for h in (0, 1):
                out.append(f(self.part(j, 0, h)) + f(self.buf.at[j, 2 + h]) + f(self.buf.at[j, 4 + h]))
            return out

    xr = Ring("x", lambda j, i: t.at[j, i % 4], xb, xs, lambda s: p.dev(dx=s), 128)
    yr = Ring("y", lambda d, i: pv_ref.at[p.row(i, d)], yb, ys, lambda s: p.dev(dy=s), 64)

    def s1(j):
        net.recv(("p", j), pb.at[j], p.dev(dk=1))
        zj = wrap(p.zh + DZ[j])
        for i in (2, 1, 3, 0):
            xa = wrap(p.x + i)
            t[j, i] = (pu_ref[p.k, zj, xa].astype(F32) + pb[j, xa].astype(F32)).astype(BF16)
        xr.open(j)

    def s3(j):
        a, b = xr.close(j)
        if j == 0:
            w0[0], w0[1] = a, b
        else:
            w[j, 0], w[j, 1] = a.astype(BF16), b.astype(BF16)
        if j == 3:
            net.send(("z", 1, "far"), w.at[3, 0], zb.at[0], p.dev(dz=1))
            net.send(("z", -1, "far"), w.at[3, 1], zb.at[1], p.dev(dz=-1))
        if j == 2:
            net.send(("z", 1, "near"), w.at[2, 1], zb.at[3], p.dev(dz=1))
        if j == 1:
            net.send(("z", -1, "near"), w.at[1, 0], zb.at[2], p.dev(dz=-1))

    steps = [0]

    def share(dev_of, mine):
        n = steps[0]
        steps[0] += 1
        for d in (1, 2, 3):
            net.send(("lo", n, d), mine, lb.at[n, d], dev_of(d))

    def shared(dev_of, mine):
        n = steps[0] - 1
        for d in (1, 2, 3):
            net.recv(("lo", n, d), lb.at[n, d], dev_of(d))
        total = (mine[...] + lb[n, 2]) + (lb[n, 1] + lb[n, 3])
        ln[n + 1] = total
        return ln.at[n + 1]

    xdev, ydev, ldev, zdev = (lambda d: p.dev(dx=d)), (lambda d: p.dev(dy=d)), (lambda d: p.dev(dl=d)), (lambda d: p.dev(dz=d))

    for d in (0, 1, 2, 3):
        yr.open(d)
    net.recv(("lp",), le.at[0], p.dev(dk=1))
    ln[0] = ls_ref[...] + le[0]
    part = ln.at[0]
    share(xdev, part)
    s1(3)
    s1(1)
    part = shared(xdev, part)
    share(ydev, part)
    for d in (2, 1, 3, 0):
        yr.middle(d)
    xr.middle(3)
    s1(2)
    s3(3)
    xr.middle(1)
    s1(0)
    part = shared(ydev, part)
    share(ldev, part)
    xr.middle(2)
    for d in (2, 1, 3):
        a, b = yr.close(d)
        wl[d, pl.ds(0, 64)], wl[d, pl.ds(64, 64)] = a.astype(BF16), b.astype(BF16)
        net.send(("l", d), wl.at[d], wl0.at[d], p.dev(dl=d))
    s3(1)
    s3(2)
    xr.middle(0)
    part = shared(ldev, part)
    share(zdev, part)
    for s, h, j in ((1, 0, 2), (-1, 1, 1)):
        net.recv(("z", s, "far"), zb.at[h], p.dev(dz=s))
        zs[h] = (f(w.at[j, h]) + f(zb.at[h])).astype(BF16)
        net.send(("z", s, "mid"), zs.at[h], zb.at[4 + h], p.dev(dz=s))
    s3(0)
    a, b = yr.close(0)
    for d in (1, 2, 3):
        net.recv(("l", d), wl0.at[d], p.dev(dl=d))
    for h, mine in ((0, a), (1, b)):
        rows = pl.ds(h * 64, 64)
        grad = mine + f(wl0.at[1, rows]) + f(wl0.at[2, rows]) + f(wl0.at[3, rows])
        old = fv_ref[rows]
        nv_ref[rows] = old - STEP * (grad + RIDGE * old)
    part = shared(zdev, part)
    loss_ref[0, 0] = jnp.sum(part[...]) * (1.0 / entries)
    for s, h in ((1, 1), (-1, 0)):
        net.recv(("z", s, "near"), zb.at[2 + h], p.dev(dz=s))
    for s, h in ((1, 0), (-1, 1)):
        net.recv(("z", s, "mid"), zb.at[4 + h], p.dev(dz=s))
        rows = pl.ds(h * 128, 128)
        grad = w0[h] + f(zb.at[2 + h]) + f(zb.at[4 + h])
        old = fu_ref[rows]
        nu_ref[rows] = old - STEP * (grad + RIDGE * old)
    net.finish()


def vmem():
    return pl.BlockSpec(memory_space=pltpu.VMEM)


def sems(n):
    return [pltpu.SemaphoreType.DMA((n,)), pltpu.SemaphoreType.DMA((n,))]


def per_device(factor_u, factor_v, values, mask_words, tile_cols):
    fu, fv = factor_u[0], factor_v[0]
    u_band, v_band, ridge = pl.pallas_call(
        gather_kernel,
        out_shape=(jax.ShapeDtypeStruct((32, 256, 128), BF16), jax.ShapeDtypeStruct((16, 128, 128), BF16),
                   jax.ShapeDtypeStruct((8, 128), F32)),
        in_specs=[vmem(), vmem()],
        out_specs=(vmem(), vmem(), vmem()),
        scratch_shapes=sems(N_GATHER),
        compiler_params=pltpu.CompilerParams(collective_id=0, has_side_effects=True),
        name="gather",
    )(fu, fv)
    pu, pv, ls = pl.pallas_call(
        compute_kernel,
        grid_spec=pltpu.PrefetchScalarGridSpec(
            num_scalar_prefetch=1,
            grid=(32 // GROUP,),
            in_specs=[
                vmem(),
                vmem(),
                pl.BlockSpec((GROUP, 256, 256), lambda g, ids: (g, 0, 0)),
                pl.BlockSpec((GROUP, 16, 256), lambda g, ids: (g, 0, 0)),
                vmem(),
            ],
            out_specs=(
                pl.BlockSpec((2, 1, 2, 256, 128), lambda g, ids: (0, lax.div(g, 2), lax.rem(g, 2), 0, 0)),
                vmem(),
                vmem(),
            ),
            scratch_shapes=[pltpu.VMEM((8, 128, 256), F32), pltpu.VMEM((8, 256), F32)],
        ),
        out_shape=(jax.ShapeDtypeStruct((2, 4, 4, 256, 128), BF16), jax.ShapeDtypeStruct((8, 256, 128), BF16),
                   jax.ShapeDtypeStruct((8, 128), F32)),
        compiler_params=pltpu.CompilerParams(dimension_semantics=("arbitrary",)),
        name="tiles",
    )(tile_cols[0, 0], u_band, v_band.reshape(8, 256, 128), values[0, 0], mask_words[0, 0], ridge)
    entries = lax.axis_size("rows") * lax.axis_size("cols") * 32 * 256 * 256
    new_u, new_v, loss = pl.pallas_call(
        lambda *refs: reduce_kernel(entries, *refs),
        out_shape=(jax.ShapeDtypeStruct((256, 128), F32), jax.ShapeDtypeStruct((128, 128), F32),
                   jax.ShapeDtypeStruct((1, 1), F32)),
        in_specs=[vmem()] * 5,
        out_specs=(vmem(), vmem(), pl.BlockSpec(memory_space=pltpu.SMEM)),
        scratch_shapes=[
            pltpu.VMEM((4, 4, 256, 128), BF16),
            pltpu.VMEM((4, 4, 256, 128), BF16),
            pltpu.VMEM((4, 6, 128, 128), BF16),
            pltpu.VMEM((4, 2, 128, 128), BF16),
            pltpu.VMEM((4, 2, 128, 128), BF16),
            pltpu.VMEM((2, 128, 128), F32),
            pltpu.VMEM((6, 128, 128), BF16),
            pltpu.VMEM((2, 128, 128), BF16),
            pltpu.VMEM((4, 6, 64, 128), BF16),
            pltpu.VMEM((4, 2, 64, 128), BF16),
            pltpu.VMEM((4, 128, 128), BF16),
            pltpu.VMEM((4, 128, 128), BF16),
            pltpu.VMEM((4, 4, 8, 128), F32),
            pltpu.VMEM((1, 8, 128), F32),
            pltpu.VMEM((5, 8, 128), F32),
            *sems(N_REDUCE),
        ],
        compiler_params=pltpu.CompilerParams(collective_id=1, has_side_effects=True),
        name="reduce",
    )(pu, pv.reshape(16, 128, 128), ls, fu, fv)
    return new_u[None], new_v[None], loss[0, 0]


def solution(mesh):
    return jax.shard_map(
        per_device,
        mesh=mesh,
        in_specs=(
            P("rows", "cols", None),
            P("cols", "rows", None),
            P("rows", "cols", None, None, None),
            P("rows", "cols", None, None, None),
            P("rows", "cols", None),
        ),
        out_specs=(P("rows", "cols", None), P("cols", "rows", None), P()),
        check_vma=False,
    )
```

time: 257 us -> 94.6 us (0.37)
  waiting for transfers between devices: 102 us -> 0 us
  Pallas kernels: 0 us -> 88.6 us
  blocking collectives: 53.9 us -> 0 us
  local copies, waits for them, and re-layouts: 45 us -> 3.04 us
  between operations: 19.7 us -> 2.38 us
  matrix products: 16.1 us -> 0 us
  starting transfers between devices: 13.6 us -> 0 us
  other arithmetic: 6.22 us -> 0 us
    pallas_call x0 -> x3, Pallas kernels: none -> 88.6 us  [the longest x1 44.7 us: per_device(): pl.pallas_call(gather_kernel, out_shape=(jax.ShapeDtypeStruct((32, 256, 1...]
    reduce_scatter x2 -> x0, waiting for transfers between devices: 61.2 us -> none  [the longest x1 59.9 us: sum_by_chip(): return lax.psum_scatter(tiles, chips, scatter_dimension=0, tiled=True)[0]]
    psum x5 -> x0, blocking collectives: 53.9 us -> none  [by_axis(): array = lax.psum(array, axis)]
    all_gather x1 -> x0, waiting for transfers between devices: 40.2 us -> none  [per_device(): u_band = lax.all_gather(u_low, COLS, axis=0, tiled=True)]
    shift_right_arithmetic x11 -> x0, local copies, waits for them, and re-layouts: 16.8 us -> none  [decode(): jnp.right_shift(mask_bits[:, :, None, :], shifts[None, None, :, None])]
    dot_general x16 -> x0, matrix products: 16.1 us -> none  [the longest x4 5.97 us: slot_terms(): jnp.einsum('sik,sjk->sij', left_rows, right_rows, preferred_element_type=...]
    all_to_all x2 -> x0, starting transfers between devices: 13.5 us -> none  [the longest x1 9.17 us: from_everyone(): return lax.all_to_all(copies, axis, split_axis=0, concat_axis=0, tiled=True)]
    unnamed x50 -> x2, local copies, waits for them, and re-layouts: 13.2 us -> 3.04 us
  transfers between devices with their start and end apart: 5 -> 0, of which waited for: 3 -> 0; matrix products, arithmetic and copies ran while one was open for 18% -> 0% of each run, Pallas kernels for 0% -> 0%
where the time goes in v1:
time: 94.6 us; the launch traced here: 94 us
  Pallas kernels  88.6 us (94%)
  local copies, waits for them, and re-layouts  3.04 us (3%)
  between operations  2.38 us (3%)
    pallas_call x1, Pallas kernels, per_device(): pl.pallas_call(gather_kernel, out_shape=(jax.ShapeDtypeStruct((32, 256, 1...  44.7 us
    pallas_call x1, Pallas kernels, per_device(): pl.pallas_call(lambda *refs: reduce_kernel(entries, *refs), out_shape=(ja...  32.1 us
    pallas_call x1, Pallas kernels, per_device(): pl.pallas_call(compute_kernel, grid_spec=pltpu.PrefetchScalarGridSpec(num...  11.7 us
    unnamed x2, local copies, waits for them, and re-layouts  3.04 us

profile of v1, /device:TPU:1, one launch (start us, length us, event | category | flops | bytes accessed | tf_op | source)
XLA Modules:
  0.0 94.0 jit_solution(7522979217743847786)
XLA Ops:
  0.6 44.7 %gather.1 = (bf16[32,256,128]{2,1,0:T(8,128)(2,1)}, bf16[16,128,128]{2,1,0:T(8,128)(2,1)}, f32[8,128]{1,0:T(8,128)}) custom-call(f32[256,128]{1,0:T(8,128)} %bitcast.13, f32[128,128]{1,0:T(8,128)} %bitcast.16), custom_call_target="tpu_custom_call" | custom-call | tf_op jit(solution)/shard_map/gather/pallas_call | solution.py:372
  45.4 11.7 %tiles.1 = (bf16[2,4,4,256,128]{4,3,2,1,0:T(8,128)(2,1)}, bf16[8,256,128]{2,1,0:T(8,128)(2,1)}, f32[8,128]{1,0:T(8,128)}) custom-call(s32[32]{0:T(128)} %bitcast.20, bf16[32,256,128]{2,1,0:T(8,128)(2,1)} %get-tuple-element.12.u_ref, bf16[8,256,128]{2,1,0:T(8,128)(2,1)} %bitcast.12, bf16[32,256,256]{2,1,0:T(8,128)(2,1)} %bitcast.10, s32[32,16,256]{2,1,0:T(8,128)} %bitcast.11, ...), custom_call_target="tpu_custom_call" | custom-call | tf_op jit(solution)/shard_map/tiles/pallas_call | solution.py:382
  57.1 32.1 %reduce.1 = (f32[256,128]{1,0:T(8,128)}, f32[128,128]{1,0:T(8,128)}, f32[1,1]{1,0:T(1,128)}) custom-call(bf16[2,4,4,256,128]{4,3,2,1,0:T(8,128)(2,1)} %get-tuple-element.15.refs_0_, bf16[16,128,128]{2,1,0:T(8,128)(2,1)} %bitcast.15, f32[8,128]{1,0:T(8,128)} %get-tuple-element.17.refs_2_, f32[256,128]{1,0:T(8,128)} %bitcast.14, f32[128,128]{1,0:T(8,128)} %bitcast.17), custom_call_target="tpu_custom_call" | custom-call | tf_op jit(solution)/shard_map/reduce/pallas_call | solution.py:407
  89.2 1.6 %copy.11 = f32[1,256,128]{2,1,0:T(8,128)} copy(f32[1,256,128]{2,1,0:T(8,128)} %bitcast.18) | data formatting | bytes 262144
  90.8 1.5 %copy.12 = f32[1,128,128]{2,1,0:T(8,128)} copy(f32[1,128,128]{2,1,0:T(8,128)} %bitcast.19) | data formatting | bytes 131072

commit v2 on v1

v2 whole, which is shorter than its diff:
```python
import jax
import jax.numpy as jnp
from jax import lax
from jax.experimental import pallas as pl
from jax.experimental.pallas import tpu as pltpu
from jax.sharding import PartitionSpec as P

F32 = jnp.float32
BF16 = jnp.bfloat16
STEP = 0.01
RIDGE = 0.1
MESH = pl.DeviceIdType.MESH


def wrap(i, n=4):
    return lax.rem(i + n, n)


class Place:
    def __init__(self):
        c = lax.axis_index("cols")
        r = lax.axis_index("rows")
        self.c, self.r = c, r
        self.k = lax.rem(c, 2)
        self.x = lax.rem(lax.div(c, 2), 4)
        self.zh = lax.div(c, 8)
        self.y = lax.div(r, 4)
        self.zl = lax.rem(r, 4)

    def col(self, dz=0, dx=0, dk=0):
        return wrap(self.zh + dz) * 8 + wrap(self.x + dx) * 2 + lax.rem(self.k + dk, 2)

    def row(self, dy=0, dl=0):
        return wrap(self.y + dy) * 4 + wrap(self.zl + dl)

    def dev(self, dz=0, dx=0, dk=0, dy=0, dl=0):
        if dy or dl:
            return {"rows": self.row(dy, dl)}
        return {"cols": self.col(dz, dx, dk)}


class Net:
    def __init__(self, send_sems, recv_sems):
        self.send_sems, self.recv_sems = send_sems, recv_sems
        self.ids, self.sent = {}, []

    def at(self, name):
        return self.ids.setdefault(name, len(self.ids))

    def send(self, name, src, dst, dev):
        i = self.at(name)
        copy = pltpu.make_async_remote_copy(
            src_ref=src, dst_ref=dst, send_sem=self.send_sems.at[i], recv_sem=self.recv_sems.at[i],
            device_id=dev, device_id_type=MESH)
        copy.start()
        self.sent.append(copy)

    def recv(self, name, ref, dev):
        i = self.at(name)
        pltpu.make_async_remote_copy(
            src_ref=ref, dst_ref=ref, send_sem=self.send_sems.at[i], recv_sem=self.recv_sems.at[i],
            device_id=dev, device_id_type=MESH).wait_recv()

    def finish(self):
        for copy in self.sent:
            copy.wait_send()


def greet(devs):
    barrier = pltpu.get_barrier_semaphore()
    for dev in devs:
        pl.semaphore_signal(barrier, inc=1, device_id=dev, device_id_type=MESH)
    pl.semaphore_wait(barrier, len(devs))


DZ = (0, -1, 1, 2)
N_COPIES = 184


def fused_kernel(entries, fu_ref, fv_ref, vals_hbm, mask_hbm, ids_ref, nu_ref, nv_ref, loss_ref,
                 u, v, vals, mask, prev, chain, pu, pv, ls, pb, t, xb, xs, w, w0, zb, zs, yb, ys, wl, wl0, lb, le, ln,
                 load_sems, send_sems, recv_sems):
    p = Place()
    net = Net(send_sems, recv_sems)

    def f(ref):
        return ref[...].astype(F32)

    loads = []
    for j in range(4):
        base = wrap(p.zh + DZ[j]) * 8
        for n, (far, near) in enumerate(((mask_hbm, mask), (vals_hbm, vals))):
            copy = pltpu.make_async_copy(far.at[pl.ds(base, 8)], near.at[pl.ds(base, 8)], load_sems.at[2 * j + n])
            copy.start()
            loads.append(copy)

    u[p.c] = fu_ref[...].astype(BF16)
    v[p.r] = fv_ref[...].astype(BF16)
    greet([p.dev(dk=1)] + [p.dev(dx=d) for d in (1, 2, 3)] + [p.dev(dz=d) for d in (1, 2, 3)]
          + [p.dev(dy=d) for d in (1, 2, 3)] + [p.dev(dl=d) for d in (1, 2, 3)])


    def ub(j, dx, h):
        return u.at[p.col(DZ[j], dx), pl.ds(h * 128, 128)]

    def vb(d, dy, h):
        return v.at[p.row(dy, d), pl.ds(h * 64, 64)]

    class Spread:
        def __init__(self, tag, view, dev):
            self.tag, self.view, self.dev = tag, view, dev

        def put(self, j, h):
            for s in ((1, -1) if h == 0 else (-1, 1)):
                ref = self.view(j, 0, h)
                net.send((self.tag, j, s, h), ref, ref, self.dev(s))

        def forward(self, j):
            for s, h in ((1, 0), (-1, 1)):
                ref = self.view(j, -s, h)
                net.recv((self.tag, j, s, h), ref, self.dev(s))
                net.send((self.tag, j, s, "hop"), ref, ref, self.dev(s))

        def finish(self, j, near=None, far=None):
            for s, h in ((1, 1), (-1, 0)):
                net.recv((self.tag, j, s, h), self.view(j, -s, h), self.dev(s))
            if near:
                near()
            for s, h in ((1, 0), (-1, 1)):
                net.recv((self.tag, j, s, "hop"), self.view(j, 2, h), self.dev(s))
            if far:
                far()

    xg = Spread("gx", ub, lambda s: p.dev(dx=s))
    yg = Spread("gy", vb, lambda s: p.dev(dy=s))

    def twin(j, dx):
        ref = u.at[p.col(DZ[j], dx)]
        net.send(("gp", j, dx), ref, ref, p.dev(dk=1))

    def xfin(j):
        xg.finish(j, lambda: (twin(j, -1), twin(j, 1)), lambda: twin(j, 2))

    def z_in(s, h, j):
        ref = ub(j, 0, h)
        net.recv(("gz", s, h), ref, p.dev(dz=s))
        if (s, h) in ((1, 0), (-1, 1)):
            net.send(("gz", s, "hop"), ref, ref, p.dev(dz=s))
        xg.put(j, h)

    def z_far():
        for s, h in ((1, 0), (-1, 1)):
            net.recv(("gz", s, "hop"), ub(3, 0, h), p.dev(dz=s))
            xg.put(3, h)
        twin(3, 0)


    order = (0, 1, 2, 3)
    probe = jnp.left_shift(1, lax.rem(lax.broadcasted_iota(jnp.int32, (16, 256), 0), 16))

    def links():
        last = [jnp.int32(-1)] * 8
        for n in range(32):
            j, m = order[n // 8], n % 8
            q = ids_ref[p.col(DZ[j], m // 2, m % 2)]
            before = jnp.int32(-1)
            for tile in range(8):
                hit = q == tile
                before = jnp.where(hit, last[tile], before)
                last[tile] = jnp.where(hit, n, last[tile])
            prev[n] = before
        for tile in range(8):
            prev[32 + tile] = last[tile]

    def linked(n):
        return jnp.where(n >= 0, chain[jnp.maximum(n, 0)], 0.0)

    def work(j, squares):
        for dx in (0, -1, 1, 2):
            net.recv(("gp", j, dx), u.at[p.col(DZ[j], dx, 1)], p.dev(dk=1))
        loads[2 * j].wait()
        loads[2 * j + 1].wait()
        zj = wrap(p.zh + DZ[j])
        first = order.index(j) * 8

        def slot(m, squares):
            i, kk = lax.div(m, 2), lax.rem(m, 2)
            s = zj * 8 + lax.rem(p.x + i, 4) * 2 + lax.rem(p.k + kk, 2)
            q = ids_ref[s]
            ut = u[s]
            vt = v[pl.ds(2 * q, 2)].reshape(256, 128)
            pred = lax.dot_general(ut, vt, (((1,), (1,)), ((), ())), preferred_element_type=F32)
            bits = jnp.concatenate(
                [jnp.bitwise_and(jnp.broadcast_to(mask[s, b:b + 1, :], (16, 256)), probe) for b in range(16)], axis=0)
            res = jnp.where(bits != 0, pred - vals[s].astype(F32), 0.0)
            low = res.astype(BF16)
            pu[j, kk, i] = jnp.dot(low, vt, preferred_element_type=F32).astype(BF16)
            chain[first + m] = linked(prev[first + m]) + lax.dot_general(
                ut, low, (((0,), (0,)), ((), ())), preferred_element_type=F32)
            return squares + jnp.sum((res * res).reshape(32, 8, 256), axis=0)

        squares = lax.fori_loop(0, 8, slot, squares)
        net.send(("p", j), pu.at[j, 1], pb.at[j], p.dev(dk=1))
        return squares


    class Ring:
        def __init__(self, tag, block, buf, mid, dev, half):
            self.tag, self.block, self.buf, self.mid, self.dev, self.half = tag, block, buf, mid, dev, half

        def part(self, j, i, h):
            return self.block(j, i).at[pl.ds(h * self.half, self.half)]

        def open(self, j):
            for s, h in ((1, 0), (-1, 1)):
                net.send((self.tag, j, s, "far"), self.part(j, 2, h), self.buf.at[j, h], self.dev(s))
            for s, h in ((1, 1), (-1, 0)):
                net.send((self.tag, j, s, "near"), self.part(j, s, h), self.buf.at[j, 2 + h], self.dev(s))

        def middle(self, j):
            for s, h in ((1, 0), (-1, 1)):
                net.recv((self.tag, j, s, "far"), self.buf.at[j, h], self.dev(s))
                self.mid[j, h] = (f(self.part(j, s, h)) + f(self.buf.at[j, h])).astype(BF16)
                net.send((self.tag, j, s, "mid"), self.mid.at[j, h], self.buf.at[j, 4 + h], self.dev(s))

        def close(self, j):
            out = []
            for s, h in ((1, 1), (-1, 0)):
                net.recv((self.tag, j, s, "near"), self.buf.at[j, 2 + h], self.dev(s))
            for s, h in ((1, 0), (-1, 1)):
                net.recv((self.tag, j, s, "mid"), self.buf.at[j, 4 + h], self.dev(s))
            for h in (0, 1):
                out.append(f(self.part(j, 0, h)) + f(self.buf.at[j, 2 + h]) + f(self.buf.at[j, 4 + h]))
            return out

    xr = Ring("x", lambda j, i: t.at[j, i % 4], xb, xs, lambda s: p.dev(dx=s), 128)
    yr = Ring("y", lambda d, i: pv.at[p.row(i, d)], yb, ys, lambda s: p.dev(dy=s), 64)

    def s1(j):
        net.recv(("p", j), pb.at[j], p.dev(dk=1))
        for i in (2, 1, 3, 0):
            t[j, i] = (pu[j, 0, i].astype(F32) + pb[j, i].astype(F32)).astype(BF16)
        xr.open(j)

    def s3(j):
        a, b = xr.close(j)
        if j == 0:
            w0[0], w0[1] = a, b
        else:
            w[j, 0], w[j, 1] = a.astype(BF16), b.astype(BF16)
        if j == 3:
            net.send(("z", 1, "far"), w.at[3, 0], zb.at[0], p.dev(dz=1))
            net.send(("z", -1, "far"), w.at[3, 1], zb.at[1], p.dev(dz=-1))
        if j == 2:
            net.send(("z", 1, "near"), w.at[2, 1], zb.at[3], p.dev(dz=1))
        if j == 1:
            net.send(("z", -1, "near"), w.at[1, 0], zb.at[2], p.dev(dz=-1))

    def share(n, dev_of):
        for d in (1, 2, 3):
            net.send(("lo", n, d), ln.at[n], lb.at[n, d], dev_of(d))

    def shared(n, dev_of):
        for d in (1, 2, 3):
            net.recv(("lo", n, d), lb.at[n, d], dev_of(d))
        ln[n + 1] = (ln[n] + lb[n, 2]) + (lb[n, 1] + lb[n, 3])

    axes = (lambda d: p.dev(dx=d), lambda d: p.dev(dy=d), lambda d: p.dev(dl=d), lambda d: p.dev(dz=d))


    for s, h in ((1, 0), (-1, 1), (1, 1), (-1, 0)):
        ref = ub(0, 0, h)
        net.send(("gz", s, h), ref, ref, p.dev(dz=s))
    for d in (1, 2, 3):
        ref = v.at[p.r]
        net.send(("gl", d), ref, ref, p.dev(dl=d))
    for h in (0, 1):
        xg.put(0, h)
    for h in (0, 1):
        yg.put(0, h)
    twin(0, 0)
    fu = fu_ref[...]
    fv = fv_ref[...]
    ridge = (0.5 * RIDGE) * (
        jnp.sum((fu * fu).reshape(32, 8, 128), axis=0) + jnp.sum((fv * fv).reshape(16, 8, 128), axis=0))
    links()
    xg.forward(0)
    yg.forward(0)
    for d in (1, 2, 3):
        net.recv(("gl", d), v.at[p.row(0, -d)], p.dev(dl=d))
        for h in (0, 1):
            yg.put(-d, h)
    xfin(0)
    z_in(1, 0, 1)
    z_in(-1, 1, 2)
    for d in (1, 2, 3):
        yg.forward(-d)
    z_in(1, 1, 1)
    z_in(-1, 0, 2)
    twin(1, 0)
    twin(2, 0)
    xg.forward(1)
    xg.forward(2)
    yg.finish(0)
    for d in (1, 2, 3):
        yg.finish(-d)
    squares = jnp.zeros((8, 256), F32)
    squares = work(0, squares)
    z_far()
    xfin(1)
    xfin(2)
    squares = work(1, squares)
    xg.forward(3)
    squares = work(2, squares)
    xfin(3)
    s1(0)
    s1(1)
    squares = work(3, squares)
    ls[...] = 0.5 * (squares[:, :128] + squares[:, 128:]) + ridge
    net.send(("lp",), ls, le.at[0], p.dev(dk=1))
    xr.middle(0)
    xr.middle(1)
    s1(2)
    for q in range(8):
        pv[pl.ds(2 * q, 2)] = linked(prev[32 + q]).T.astype(BF16).reshape(2, 128, 128)
    for d in (0, 1, 2, 3):
        yr.open(d)
    s1(3)
    s3(1)
    xr.middle(2)
    net.recv(("lp",), le.at[0], p.dev(dk=1))
    ln[0] = ls[...] + le[0]
    share(0, axes[0])
    for d in (2, 1, 3, 0):
        yr.middle(d)
    xr.middle(3)
    s3(2)
    shared(0, axes[0])
    share(1, axes[1])
    s3(3)
    for d in (2, 1, 3):
        a, b = yr.close(d)
        wl[d, pl.ds(0, 64)], wl[d, pl.ds(64, 64)] = a.astype(BF16), b.astype(BF16)
        net.send(("l", d), wl.at[d], wl0.at[d], p.dev(dl=d))
    shared(1, axes[1])
    share(2, axes[2])
    s3(0)
    shared(2, axes[2])
    share(3, axes[3])
    for s, h, j in ((1, 0, 2), (-1, 1, 1)):
        net.recv(("z", s, "far"), zb.at[h], p.dev(dz=s))
        zs[h] = (f(w.at[j, h]) + f(zb.at[h])).astype(BF16)
        net.send(("z", s, "mid"), zs.at[h], zb.at[4 + h], p.dev(dz=s))
    a, b = yr.close(0)
    for d in (1, 2, 3):
        net.recv(("l", d), wl0.at[d], p.dev(dl=d))
    for h, mine in ((0, a), (1, b)):
        rows = pl.ds(h * 64, 64)
        grad = mine + f(wl0.at[1, rows]) + f(wl0.at[2, rows]) + f(wl0.at[3, rows])
        old = fv_ref[rows]
        nv_ref[rows] = old - STEP * (grad + RIDGE * old)
    shared(3, axes[3])
    loss_ref[0, 0] = jnp.sum(ln[4]) * (1.0 / entries)
    for s, h in ((1, 1), (-1, 0)):
        net.recv(("z", s, "near"), zb.at[2 + h], p.dev(dz=s))
    for s, h in ((1, 0), (-1, 1)):
        net.recv(("z", s, "mid"), zb.at[4 + h], p.dev(dz=s))
        rows = pl.ds(h * 128, 128)
        grad = w0[h] + f(zb.at[2 + h]) + f(zb.at[4 + h])
        old = fu_ref[rows]
        nu_ref[rows] = old - STEP * (grad + RIDGE * old)
    net.finish()


def vmem():
    return pl.BlockSpec(memory_space=pltpu.VMEM)


def per_device(factor_u, factor_v, values, mask_words, tile_cols):
    entries = lax.axis_size("rows") * lax.axis_size("cols") * 32 * 256 * 256
    far = pl.BlockSpec(memory_space=pltpu.HBM)
    near = pl.BlockSpec(memory_space=pltpu.SMEM)

    def low(*shape):
        return pltpu.VMEM(shape, BF16)

    def full(*shape):
        return pltpu.VMEM(shape, F32)

    new_u, new_v, loss = pl.pallas_call(
        lambda *refs: fused_kernel(entries, *refs),
        out_shape=(jax.ShapeDtypeStruct((256, 128), F32), jax.ShapeDtypeStruct((128, 128), F32),
                   jax.ShapeDtypeStruct((1, 1), F32)),
        in_specs=[vmem(), vmem(), far, far, near],
        out_specs=(vmem(), vmem(), near),
        scratch_shapes=[
            low(32, 256, 128),
            low(16, 128, 128),
            low(32, 256, 256),
            pltpu.VMEM((32, 16, 256), jnp.int32),
            pltpu.SMEM((40,), jnp.int32),
            full(32, 128, 256),
            low(4, 2, 4, 256, 128),
            low(16, 128, 128),
            full(8, 128),
            low(4, 4, 256, 128),
            low(4, 4, 256, 128),
            low(4, 6, 128, 128),
            low(4, 2, 128, 128),
            low(4, 2, 128, 128),
            full(2, 128, 128),
            low(6, 128, 128),
            low(2, 128, 128),
            low(4, 6, 64, 128),
            low(4, 2, 64, 128),
            low(4, 128, 128),
            low(4, 128, 128),
            full(4, 4, 8, 128),
            full(1, 8, 128),
            full(5, 8, 128),
            pltpu.SemaphoreType.DMA((8,)),
            pltpu.SemaphoreType.DMA((N_COPIES,)),
            pltpu.SemaphoreType.DMA((N_COPIES,)),
        ],
        compiler_params=pltpu.CompilerParams(collective_id=0, has_side_effects=True),
        name="fused",
    )(factor_u[0], factor_v[0], values[0, 0], mask_words[0, 0], tile_cols[0, 0])
    return new_u[None], new_v[None], loss[0, 0]


def solution(mesh):
    return jax.shard_map(
        per_device,
        mesh=mesh,
        in_specs=(
            P("rows", "cols", None),
            P("cols", "rows", None),
            P("rows", "cols", None, None, None),
            P("rows", "cols", None, None, None),
            P("rows", "cols", None),
        ),
        out_specs=(P("rows", "cols", None), P("cols", "rows", None), P()),
        check_vma=False,
    )
```

time: 94.6 us -> 82.9 us (0.88)
  the two profiles are of different devices: /device:TPU:1 before, /device:TPU:6 now
where the time goes in v2:
time: 82.9 us; the launch traced here: 82.7 us
  Pallas kernels  77.2 us (93%)
  local copies, waits for them, and re-layouts  3.04 us (4%)
  between operations  2.4 us (3%)
    pallas_call x1, Pallas kernels, per_device(): pl.pallas_call(lambda *refs: fused_kernel(entries, *refs), out_shape=(jax...  77.2 us
    unnamed x2, local copies, waits for them, and re-layouts  3.04 us

profile of v2, /device:TPU:6, one launch (start us, length us, event | category | flops | bytes accessed | tf_op | source)
XLA Modules:
  0.0 82.7 jit_solution(167679648047622813)
XLA Ops:
  0.6 77.2 %fused.1 = (f32[256,128]{1,0:T(8,128)}, f32[128,128]{1,0:T(8,128)}, f32[1,1]{1,0:T(1,128)}) custom-call(f32[256,128]{1,0:T(8,128)} %bitcast.10, f32[128,128]{1,0:T(8,128)} %bitcast.12, bf16[32,256,256]{2,1,0:T(8,128)(2,1)} %bitcast.8, s32[32,16,256]{2,1,0:T(8,128)} %bitcast.9, s32[32]{0:T(128)} %bitcast.14), custom_call_target="tpu_custom_call" | custom-call | tf_op jit(solution)/shard_map/fused/pallas_call | solution.py:390
  77.9 1.6 %copy.11 = f32[1,256,128]{2,1,0:T(8,128)} copy(f32[1,256,128]{2,1,0:T(8,128)} %bitcast.11) | data formatting | bytes 262144
  79.4 1.5 %copy.12 = f32[1,128,128]{2,1,0:T(8,128)} copy(f32[1,128,128]{2,1,0:T(8,128)} %bitcast.13) | data formatting | bytes 131072

commit v3 on v2

v3 whole, which is shorter than its diff:
```python
import jax
import jax.numpy as jnp
from jax import lax
from jax.experimental import pallas as pl
from jax.experimental.pallas import tpu as pltpu
from jax.sharding import PartitionSpec as P

F32 = jnp.float32
BF16 = jnp.bfloat16
STEP = 0.01
RIDGE = 0.1
MESH = pl.DeviceIdType.MESH


def wrap(i, n=4):
    return lax.rem(i + n, n)


class Place:
    def __init__(self):
        c = lax.axis_index("cols")
        r = lax.axis_index("rows")
        self.c, self.r = c, r
        self.k = lax.rem(c, 2)
        self.x = lax.rem(lax.div(c, 2), 4)
        self.zh = lax.div(c, 8)
        self.y = lax.div(r, 4)
        self.zl = lax.rem(r, 4)

    def col(self, dz=0, dx=0, dk=0):
        return wrap(self.zh + dz) * 8 + wrap(self.x + dx) * 2 + lax.rem(self.k + dk, 2)

    def row(self, dy=0, dl=0):
        return wrap(self.y + dy) * 4 + wrap(self.zl + dl)

    def dev(self, dz=0, dx=0, dk=0, dy=0, dl=0):
        if dy or dl:
            return {"rows": self.row(dy, dl)}
        return {"cols": self.col(dz, dx, dk)}


class Net:
    def __init__(self, send_sems, recv_sems):
        self.send_sems, self.recv_sems = send_sems, recv_sems
        self.ids, self.sent = {}, []

    def at(self, name):
        return self.ids.setdefault(name, len(self.ids))

    def send(self, name, src, dst, dev):
        i = self.at(name)
        copy = pltpu.make_async_remote_copy(
            src_ref=src, dst_ref=dst, send_sem=self.send_sems.at[i], recv_sem=self.recv_sems.at[i],
            device_id=dev, device_id_type=MESH)
        copy.start()
        self.sent.append(copy)

    def recv(self, name, ref, dev):
        i = self.at(name)
        pltpu.make_async_remote_copy(
            src_ref=ref, dst_ref=ref, send_sem=self.send_sems.at[i], recv_sem=self.recv_sems.at[i],
            device_id=dev, device_id_type=MESH).wait_recv()

    def finish(self):
        for copy in self.sent:
            copy.wait_send()


DZ = (0, -1, 1, 2)
N_COPIES = 120
UNROLL = 4


def fused_kernel(entries, fu_hbm, fv_hbm, vals_hbm, mask_hbm, ids_ref, nu_ref, nv_ref, loss_ref,
                 fu_ref, fv_ref, u, v, vals, mask, prev, chain, pu, pv, ls, pb, t, xb, w, w0, zb, yb, wl, wl0, lb, le, ln,
                 load_sems, send_sems, recv_sems):
    p = Place()
    net = Net(send_sems, recv_sems)

    def f(ref):
        return ref[...].astype(F32)

    own = [pltpu.make_async_copy(fu_hbm, fu_ref, load_sems.at[8]), pltpu.make_async_copy(fv_hbm, fv_ref, load_sems.at[9])]
    for copy in own:
        copy.start()
    loads = []
    for j in range(4):
        base = wrap(p.zh + DZ[j]) * 8
        for n, (far, near) in enumerate(((mask_hbm, mask), (vals_hbm, vals))):
            copy = pltpu.make_async_copy(far.at[pl.ds(base, 8)], near.at[pl.ds(base, 8)], load_sems.at[2 * j + n])
            copy.start()
            loads.append(copy)

    peers = ([p.dev(dk=1)] + [p.dev(dx=d) for d in (1, 2, 3)] + [p.dev(dz=d) for d in (1, 2, 3)]
             + [p.dev(dy=d) for d in (1, 2, 3)] + [p.dev(dl=d) for d in (1, 2, 3)])
    barrier = pltpu.get_barrier_semaphore()
    for peer in peers:
        pl.semaphore_signal(barrier, inc=1, device_id=peer, device_id_type=MESH)
    for copy in own:
        copy.wait()
    u[p.c] = fu_ref[...].astype(BF16)
    v[p.r] = fv_ref[...].astype(BF16)
    pl.semaphore_wait(barrier, len(peers))


    def ub(j, dx, h):
        return u.at[p.col(DZ[j], dx), pl.ds(h * 128, 128)]

    def xput(j, h):
        for d in (1, -1, 2):
            ref = ub(j, 0, h)
            net.send(("gx", j, d, h), ref, ref, p.dev(dx=d))

    def xin(j, d):
        for h in (0, 1):
            net.recv(("gx", j, d, h), ub(j, -d, h), p.dev(dx=d))
        twin(j, -d)

    def yput(l):
        ref = v.at[p.row(0, l)]
        for d in (1, -1, 2):
            net.send(("gy", l, d), ref, ref, p.dev(dy=d))

    def yin(l):
        for d in (1, -1, 2):
            net.recv(("gy", l, d), v.at[p.row(-d, l)], p.dev(dy=d))

    def twin(j, dx):
        dx %= 4
        ref = u.at[p.col(DZ[j], dx)]
        net.send(("gp", j, dx), ref, ref, p.dev(dk=1))

    def z_in(s, h, j):
        ref = ub(j, 0, h)
        net.recv(("gz", s, h), ref, p.dev(dz=s))
        if (s, h) in ((1, 0), (-1, 1)):
            net.send(("gz", s, "hop"), ref, ref, p.dev(dz=s))
        xput(j, h)

    def z_far():
        for s, h in ((1, 0), (-1, 1)):
            net.recv(("gz", s, "hop"), ub(3, 0, h), p.dev(dz=s))
            xput(3, h)
        twin(3, 0)


    order = (0, 1, 2, 3)
    probe = jnp.left_shift(1, lax.rem(lax.broadcasted_iota(jnp.int32, (16, 256), 0), 16))

    def links():
        last = [jnp.int32(-1)] * 8
        for n in range(32):
            j, i = order[n // 8], (0, 1, 3, 2)[n % 8 // 2]
            q = ids_ref[p.col(DZ[j], i, n % 2)]
            before = jnp.int32(-1)
            for tile in range(8):
                hit = q == tile
                before = jnp.where(hit, last[tile], before)
                last[tile] = jnp.where(hit, n, last[tile])
            prev[n] = before
        for tile in range(8):
            prev[32 + tile] = last[tile]

    def linked(n):
        return jnp.where(n >= 0, chain[jnp.maximum(n, 0)], 0.0)

    def work(j, part, squares):
        for dx in ((0, 1), (3, 2))[part]:
            net.recv(("gp", j, dx), u.at[p.col(DZ[j], dx, 1)], p.dev(dk=1))
        if part == 0:
            loads[2 * j].wait()
            loads[2 * j + 1].wait()
        zj = wrap(p.zh + DZ[j])
        first = order.index(j) * 8 + 4 * part

        def slot(m, squares):
            i = lax.div(m, 2) if part == 0 else 3 - lax.div(m, 2)
            kk = lax.rem(m, 2)
            s = zj * 8 + lax.rem(p.x + i, 4) * 2 + lax.rem(p.k + kk, 2)
            q = ids_ref[s]
            ut = u[s]
            vt = v[pl.ds(2 * q, 2)].reshape(256, 128)
            pred = lax.dot_general(ut, vt, (((1,), (1,)), ((), ())), preferred_element_type=F32)
            bits = jnp.concatenate(
                [jnp.bitwise_and(jnp.broadcast_to(mask[s, b:b + 1, :], (16, 256)), probe) for b in range(16)], axis=0)
            res = jnp.where(bits != 0, pred - vals[s].astype(F32), 0.0)
            low = res.astype(BF16)
            pu[j, kk, i] = jnp.dot(low, vt, preferred_element_type=F32).astype(BF16)
            chain[first + m] = linked(prev[first + m]) + lax.dot_general(
                ut, low, (((0,), (0,)), ((), ())), preferred_element_type=F32)
            return squares + jnp.sum((res * res).reshape(32, 8, 256), axis=0)

        squares = lax.fori_loop(0, 4, slot, squares, unroll=UNROLL)
        rows = pl.ds(2 * part, 2)
        net.send(("p", j, part), pu.at[j, 1, rows], pb.at[j, rows], p.dev(dk=1))
        return squares


    def s1(j):
        for part in (0, 1):
            rows = pl.ds(2 * part, 2)
            net.recv(("p", j, part), pb.at[j, rows], p.dev(dk=1))
        for i in (2, 1, 3):
            t[j, i] = (f(pu.at[j, 0, i]) + f(pb.at[j, i])).astype(BF16)
            net.send(("x", j, i), t.at[j, i], xb.at[j, i], p.dev(dx=i))
        xb[j, 0] = (f(pu.at[j, 0, 0]) + f(pb.at[j, 0])).astype(BF16)

    def s3(j):
        for i in (1, 3, 2):
            net.recv(("x", j, i), xb.at[j, i], p.dev(dx=i))
        total = (f(xb.at[j, 0]) + f(xb.at[j, 1])) + (f(xb.at[j, 2]) + f(xb.at[j, 3]))
        if j == 0:
            w0[...] = total
        else:
            w[j] = total.astype(BF16)
            net.send(("z", j), w.at[j], zb.at[j], p.dev(dz=DZ[j]))

    def yopen(l):
        for i in (2, 1, 3):
            net.send(("y", l, i), pv.at[p.row(i, l)], yb.at[l, i], p.dev(dy=i))

    def yclose(l):
        for i in (1, 3, 2):
            net.recv(("y", l, i), yb.at[l, i], p.dev(dy=i))
        total = (f(pv.at[p.row(0, l)]) + f(yb.at[l, 1])) + (f(yb.at[l, 2]) + f(yb.at[l, 3]))
        if l:
            wl[l] = total.astype(BF16)
            net.send(("l", l), wl.at[l], wl0.at[l], p.dev(dl=l))
        return total

    def share(n, dev_of):
        for d in (1, 2, 3):
            net.send(("lo", n, d), ln.at[n], lb.at[n, d], dev_of(d))

    def shared(n, dev_of):
        for d in (1, 2, 3):
            net.recv(("lo", n, d), lb.at[n, d], dev_of(d))
        ln[n + 1] = (ln[n] + lb[n, 2]) + (lb[n, 1] + lb[n, 3])

    axes = (lambda d: p.dev(dz=d), lambda d: p.dev(dx=d), lambda d: p.dev(dy=d), lambda d: p.dev(dl=d))


    for d in (1, 2, 3):
        ref = v.at[p.r]
        net.send(("gl", d), ref, ref, p.dev(dl=d))
    yput(0)
    for s, h in ((1, 0), (-1, 1), (1, 1), (-1, 0)):
        ref = ub(0, 0, h)
        net.send(("gz", s, h), ref, ref, p.dev(dz=s))
    for h in (0, 1):
        xput(0, h)
    twin(0, 0)
    fu = fu_ref[...]
    fv = fv_ref[...]
    ridge = (0.5 * RIDGE) * (
        jnp.sum((fu * fu).reshape(32, 8, 128), axis=0) + jnp.sum((fv * fv).reshape(16, 8, 128), axis=0))
    links()
    for d in (1, 3, 2):
        net.recv(("gl", d), v.at[p.row(0, -d)], p.dev(dl=d))
        yput(-d)
    for d in (1, -1, 2):
        xin(0, d)
    z_in(1, 0, 1)
    z_in(-1, 1, 2)
    z_in(1, 1, 1)
    z_in(-1, 0, 2)
    twin(1, 0)
    twin(2, 0)
    for d in (0, 1, 2, 3):
        yin(-d)
    squares = jnp.zeros((8, 256), F32)
    squares = work(0, 0, squares)
    squares = work(0, 1, squares)
    for d in (-1, 1, 2):
        xin(1, d)
    z_far()
    squares = work(1, 0, squares)
    for d in (-1, 1, 2):
        xin(2, d)
    squares = work(1, 1, squares)
    squares = work(2, 0, squares)
    s1(1)
    squares = work(2, 1, squares)
    xin(3, -1)
    xin(3, 1)
    s1(2)
    squares = work(3, 0, squares)
    xin(3, 2)
    s3(1)
    squares = work(3, 1, squares)
    ls[...] = 0.5 * (squares[:, :128] + squares[:, 128:]) + ridge
    net.send(("lp",), ls, le.at[0], p.dev(dk=1))
    for q in range(8):
        pv[pl.ds(2 * q, 2)] = linked(prev[32 + q]).T.astype(BF16).reshape(2, 128, 128)
    for l in (1, 2, 3, 0):
        yopen(l)
    s1(3)
    net.recv(("lp",), le.at[0], p.dev(dk=1))
    ln[0] = ls[...] + le[0]
    share(0, axes[0])
    s1(0)
    s3(2)
    s3(3)
    for l in (1, 2, 3):
        yclose(l)
    mine = yclose(0)
    shared(0, axes[0])
    share(1, axes[1])
    s3(0)
    shared(1, axes[1])
    share(2, axes[2])
    shared(2, axes[2])
    share(3, axes[3])
    for l in (1, 2, 3):
        net.recv(("l", l), wl0.at[l], p.dev(dl=l))
    grad = (mine + f(wl0.at[1])) + (f(wl0.at[2]) + f(wl0.at[3]))
    old = fv_ref[...]
    nv_ref[...] = old - STEP * (grad + RIDGE * old)
    for j in (1, 2, 3):
        net.recv(("z", j), zb.at[j], p.dev(dz=DZ[j]))
    grad = (w0[...] + f(zb.at[1])) + (f(zb.at[2]) + f(zb.at[3]))
    old = fu_ref[...]
    nu_ref[...] = old - STEP * (grad + RIDGE * old)
    shared(3, axes[3])
    loss_ref[0, 0] = jnp.sum(ln[4]) * (1.0 / entries)
    net.finish()


def vmem():
    return pl.BlockSpec(memory_space=pltpu.VMEM)


def per_device(factor_u, factor_v, values, mask_words, tile_cols):
    entries = lax.axis_size("rows") * lax.axis_size("cols") * 32 * 256 * 256
    far = pl.BlockSpec(memory_space=pltpu.HBM)
    near = pl.BlockSpec(memory_space=pltpu.SMEM)

    def low(*shape):
        return pltpu.VMEM(shape, BF16)

    def full(*shape):
        return pltpu.VMEM(shape, F32)

    new_u, new_v, loss = pl.pallas_call(
        lambda *refs: fused_kernel(entries, *refs),
        out_shape=(jax.ShapeDtypeStruct((256, 128), F32), jax.ShapeDtypeStruct((128, 128), F32),
                   jax.ShapeDtypeStruct((1, 1), F32)),
        in_specs=[far, far, far, far, near],
        out_specs=(vmem(), vmem(), near),
        scratch_shapes=[
            full(256, 128),
            full(128, 128),
            low(32, 256, 128),
            low(16, 128, 128),
            low(32, 256, 256),
            pltpu.VMEM((32, 16, 256), jnp.int32),
            pltpu.SMEM((40,), jnp.int32),
            full(32, 128, 256),
            low(4, 2, 4, 256, 128),
            low(16, 128, 128),
            full(8, 128),
            low(4, 4, 256, 128),
            low(4, 4, 256, 128),
            low(4, 4, 256, 128),
            low(4, 256, 128),
            full(256, 128),
            low(4, 256, 128),
            low(4, 4, 128, 128),
            low(4, 128, 128),
            low(4, 128, 128),
            full(4, 4, 8, 128),
            full(1, 8, 128),
            full(5, 8, 128),
            pltpu.SemaphoreType.DMA((10,)),
            pltpu.SemaphoreType.DMA((N_COPIES,)),
            pltpu.SemaphoreType.DMA((N_COPIES,)),
        ],
        compiler_params=pltpu.CompilerParams(collective_id=0, has_side_effects=True),
        name="fused",
    )(factor_u[0], factor_v[0], values[0, 0], mask_words[0, 0], tile_cols[0, 0])
    return new_u[None], new_v[None], loss[0, 0]


def solution(mesh):
    return jax.shard_map(
        per_device,
        mesh=mesh,
        in_specs=(
            P("rows", "cols", None),
            P("cols", "rows", None),
            P("rows", "cols", None, None, None),
            P("rows", "cols", None, None, None),
            P("rows", "cols", None),
        ),
        out_specs=(P("rows", "cols", None), P("cols", "rows", None), P()),
        check_vma=False,
    )
```

time: 82.9 us -> 74.5 us (0.90)
  the two profiles are of different devices: /device:TPU:6 before, /device:TPU:1 now
where the time goes in v3:
time: 74.5 us; the launch traced here: 74.3 us
  Pallas kernels  68.9 us (92%)
  local copies, waits for them, and re-layouts  3.04 us (4%)
  between operations  2.4 us (3%)
    pallas_call x1, Pallas kernels, per_device(): pl.pallas_call(lambda *refs: fused_kernel(entries, *refs), out_shape=(jax...  68.9 us
    unnamed x2, local copies, waits for them, and re-layouts  3.04 us

profile of v3, /device:TPU:1, one launch (start us, length us, event | category | flops | bytes accessed | tf_op | source)
XLA Modules:
  0.0 74.3 jit_solution(9388603785153477727)
XLA Ops:
  0.6 68.9 %fused.1 = (f32[256,128]{1,0:T(8,128)}, f32[128,128]{1,0:T(8,128)}, f32[1,1]{1,0:T(1,128)}) custom-call(f32[256,128]{1,0:T(8,128)} %bitcast.10, f32[128,128]{1,0:T(8,128)} %bitcast.12, bf16[32,256,256]{2,1,0:T(8,128)(2,1)} %bitcast.8, s32[32,16,256]{2,1,0:T(8,128)} %bitcast.9, s32[32]{0:T(128)} %bitcast.14), custom_call_target="tpu_custom_call" | custom-call | tf_op jit(solution)/shard_map/fused/pallas_call | solution.py:344
  69.5 1.6 %copy.11 = f32[1,256,128]{2,1,0:T(8,128)} copy(f32[1,256,128]{2,1,0:T(8,128)} %bitcast.11) | data formatting | bytes 262144
  71.1 1.5 %copy.12 = f32[1,128,128]{2,1,0:T(8,128)} copy(f32[1,128,128]{2,1,0:T(8,128)} %bitcast.13) | data formatting | bytes 131072

commit v4 on v3

--- a/solution.py
+++ b/solution.py
@@ -67,12 +67,12 @@
 
 
 DZ = (0, -1, 1, 2)
-N_COPIES = 120
+N_COPIES = 140
 UNROLL = 4
 
 
 def fused_kernel(entries, fu_hbm, fv_hbm, vals_hbm, mask_hbm, ids_ref, nu_ref, nv_ref, loss_ref,
-                 fu_ref, fv_ref, u, v, vals, mask, prev, chain, pu, pv, ls, pb, t, xb, w, w0, zb, yb, wl, wl0, lb, le, ln,
+                 fu_ref, fv_ref, u, v, vals, mask, prev, chain, pu, pv, ls, pb, t, xb, w, w0, zb, yb, wl, wl0, lb, le, ln, lz, lx,
                  load_sems, send_sems, recv_sems):
     p = Place()
     net = Net(send_sems, recv_sems)
@@ -91,8 +91,12 @@
             copy.start()
             loads.append(copy)
 
-    peers = ([p.dev(dk=1)] + [p.dev(dx=d) for d in (1, 2, 3)] + [p.dev(dz=d) for d in (1, 2, 3)]
-             + [p.dev(dy=d) for d in (1, 2, 3)] + [p.dev(dl=d) for d in (1, 2, 3)])
+    def zdev(d):
+        place = lax.rem(p.zh * 4 + p.zl + d, 16)
+        return {"cols": lax.div(place, 4) * 8 + p.x * 2 + p.k, "rows": p.y * 4 + lax.rem(place, 4)}
+
+    peers = ([p.dev(dk=1)] + [p.dev(dx=d) for d in (1, 2, 3)] + [p.dev(dy=d) for d in (1, 2, 3)]
+             + [zdev(d) for d in range(1, 16)])
     barrier = pltpu.get_barrier_semaphore()
     for peer in peers:
         pl.semaphore_signal(barrier, inc=1, device_id=peer, device_id_type=MESH)
@@ -196,24 +200,33 @@
         return squares
 
 
-    def s1(j):
-        for part in (0, 1):
-            rows = pl.ds(2 * part, 2)
-            net.recv(("p", j, part), pb.at[j, rows], p.dev(dk=1))
-        for i in (2, 1, 3):
-            t[j, i] = (f(pu.at[j, 0, i]) + f(pb.at[j, i])).astype(BF16)
-            net.send(("x", j, i), t.at[j, i], xb.at[j, i], p.dev(dx=i))
-        xb[j, 0] = (f(pu.at[j, 0, 0]) + f(pb.at[j, 0])).astype(BF16)
+    halves = {0: (slice(0, 256),), 1: (slice(0, 256),), 2: (slice(0, 256),), 3: (slice(0, 128), slice(128, 256))}
+
+    def cut(j, h):
+        return pl.ds(halves[j][h].start, halves[j][h].stop - halves[j][h].start)
+
+    def s1(j, part):
+        rows = pl.ds(2 * part, 2)
+        net.recv(("p", j, part), pb.at[j, rows], p.dev(dk=1))
+        for h in range(len(halves[j])):
+            r = cut(j, h)
+            for i in ((1,), (2, 3))[part]:
+                t[j, i, r] = (f(pu.at[j, 0, i, r]) + f(pb.at[j, i, r])).astype(BF16)
+                net.send(("x", j, i, h), t.at[j, i, r], xb.at[j, i, r], p.dev(dx=i))
+        if part == 0:
+            xb[j, 0] = (f(pu.at[j, 0, 0]) + f(pb.at[j, 0])).astype(BF16)
 
     def s3(j):
-        for i in (1, 3, 2):
-            net.recv(("x", j, i), xb.at[j, i], p.dev(dx=i))
-        total = (f(xb.at[j, 0]) + f(xb.at[j, 1])) + (f(xb.at[j, 2]) + f(xb.at[j, 3]))
-        if j == 0:
-            w0[...] = total
-        else:
-            w[j] = total.astype(BF16)
-            net.send(("z", j), w.at[j], zb.at[j], p.dev(dz=DZ[j]))
+        for h in range(len(halves[j])):
+            r = cut(j, h)
+            for i in (1, 3, 2):
+                net.recv(("x", j, i, h), xb.at[j, i, r], p.dev(dx=i))
+            total = (f(xb.at[j, 0, r]) + f(xb.at[j, 1, r])) + (f(xb.at[j, 2, r]) + f(xb.at[j, 3, r]))
+            if j == 0:
+                w0[...] = total
+            else:
+                w[j, r] = total.astype(BF16)
+                net.send(("z", j, h), w.at[j, r], zb.at[j, r], p.dev(dz=DZ[j]))
 
     def yopen(l):
         for i in (2, 1, 3):
@@ -237,16 +250,21 @@
             net.recv(("lo", n, d), lb.at[n, d], dev_of(d))
         ln[n + 1] = (ln[n] + lb[n, 2]) + (lb[n, 1] + lb[n, 3])
 
-    axes = (lambda d: p.dev(dz=d), lambda d: p.dev(dx=d), lambda d: p.dev(dy=d), lambda d: p.dev(dl=d))
-
-
+    axes = (lambda d: p.dev(dx=d), lambda d: p.dev(dy=d))
+
+
+    def zput(s, h):
+        ref = ub(0, 0, h)
+        net.send(("gz", s, h), ref, ref, p.dev(dz=s))
+
+    zput(1, 0)
+    zput(-1, 1)
     for d in (1, 2, 3):
         ref = v.at[p.r]
         net.send(("gl", d), ref, ref, p.dev(dl=d))
+    zput(1, 1)
+    zput(-1, 0)
     yput(0)
-    for s, h in ((1, 0), (-1, 1), (1, 1), (-1, 0)):
-        ref = ub(0, 0, h)
-        net.send(("gz", s, h), ref, ref, p.dev(dz=s))
     for h in (0, 1):
         xput(0, h)
     twin(0, 0)
@@ -270,59 +288,69 @@
         yin(-d)
     squares = jnp.zeros((8, 256), F32)
     squares = work(0, 0, squares)
+    for d in (-1, 1):
+        xin(1, d)
     squares = work(0, 1, squares)
-    for d in (-1, 1, 2):
-        xin(1, d)
+    xin(1, 2)
     z_far()
     squares = work(1, 0, squares)
     for d in (-1, 1, 2):
         xin(2, d)
     squares = work(1, 1, squares)
     squares = work(2, 0, squares)
-    s1(1)
-    squares = work(2, 1, squares)
+    s1(1, 0)
+    s1(1, 1)
     xin(3, -1)
     xin(3, 1)
-    s1(2)
+    squares = work(2, 1, squares)
+    s1(2, 0)
+    xin(3, 2)
     squares = work(3, 0, squares)
-    xin(3, 2)
-    s3(1)
+    s1(2, 1)
     squares = work(3, 1, squares)
-    ls[...] = 0.5 * (squares[:, :128] + squares[:, 128:]) + ridge
+    ls[...] = jnp.sum(0.5 * (squares[:, :128] + squares[:, 128:]) + ridge, axis=0, keepdims=True)
     net.send(("lp",), ls, le.at[0], p.dev(dk=1))
+    s1(3, 0)
     for q in range(8):
         pv[pl.ds(2 * q, 2)] = linked(prev[32 + q]).T.astype(BF16).reshape(2, 128, 128)
     for l in (1, 2, 3, 0):
         yopen(l)
-    s1(3)
+    s1(3, 1)
     net.recv(("lp",), le.at[0], p.dev(dk=1))
-    ln[0] = ls[...] + le[0]
-    share(0, axes[0])
-    s1(0)
+    total = ls[...] + le[0]
+    here = p.zh * 4 + p.zl
+    lz[here] = total
+    lx[0] = total
+    for d in range(1, 16):
+        net.send(("lz", d), lx.at[0], lz.at[here], zdev(d))
+    s3(1)
     s3(2)
+    s1(0, 0)
+    s1(0, 1)
     s3(3)
     for l in (1, 2, 3):
         yclose(l)
     mine = yclose(0)
+    for d in range(1, 16):
+        net.recv(("lz", d), lz.at[lax.rem(here + 16 - d, 16)], zdev(d))
+    ln[0] = jnp.sum(lz[...], axis=0)
+    share(0, axes[0])
+    s3(0)
     shared(0, axes[0])
     share(1, axes[1])
-    s3(0)
-    shared(1, axes[1])
-    share(2, axes[2])
-    shared(2, axes[2])
-    share(3, axes[3])
     for l in (1, 2, 3):
         net.recv(("l", l), wl0.at[l], p.dev(dl=l))
     grad = (mine + f(wl0.at[1])) + (f(wl0.at[2]) + f(wl0.at[3]))
     old = fv_ref[...]
     nv_ref[...] = old - STEP * (grad + RIDGE * old)
+    shared(1, axes[1])
+    loss_ref[0, 0] = jnp.sum(ln[2]) * (1.0 / entries)
     for j in (1, 2, 3):
-        net.recv(("z", j), zb.at[j], p.dev(dz=DZ[j]))
+        for h in range(len(halves[j])):
+            net.recv(("z", j, h), zb.at[j, cut(j, h)], p.dev(dz=DZ[j]))
     grad = (w0[...] + f(zb.at[1])) + (f(zb.at[2]) + f(zb.at[3]))
     old = fu_ref[...]
     nu_ref[...] = old - STEP * (grad + RIDGE * old)
-    shared(3, axes[3])
-    loss_ref[0, 0] = jnp.sum(ln[4]) * (1.0 / entries)
     net.finish()
 
 
@@ -358,7 +386,7 @@
             full(32, 128, 256),
             low(4, 2, 4, 256, 128),
             low(16, 128, 128),
-            full(8, 128),
+            full(1, 128),
             low(4, 4, 256, 128),
             low(4, 4, 256, 128),
             low(4, 4, 256, 128),
@@ -368,9 +396,11 @@
             low(4, 4, 128, 128),
             low(4, 128, 128),
             low(4, 128, 128),
-            full(4, 4, 8, 128),
-            full(1, 8, 128),
-            full(5, 8, 128),
+            full(4, 4, 1, 128),
+            full(1, 1, 128),
+            full(5, 1, 128),
+            full(16, 1, 128),
+            full(1, 1, 128),
             pltpu.SemaphoreType.DMA((10,)),
             pltpu.SemaphoreType.DMA((N_COPIES,)),
             pltpu.SemaphoreType.DMA((N_COPIES,)),

time: 74.5 us -> 70.3 us (0.944)
  Pallas kernels: 68.9 us -> 64.6 us
    pallas_call x1, Pallas kernels: 68.9 us -> 64.6 us  [per_device(): pl.pallas_call(lambda *refs: fused_kernel(entries, *refs), out_shape=(jax...]
where the time goes in v4:
time: 70.3 us; the launch traced here: 70 us
  Pallas kernels  64.6 us (92%)
  local copies, waits for them, and re-layouts  3.04 us (4%)
  between operations  2.4 us (3%)
    pallas_call x1, Pallas kernels, per_device(): pl.pallas_call(lambda *refs: fused_kernel(entries, *refs), out_shape=(jax...  64.6 us
    unnamed x2, local copies, waits for them, and re-layouts  3.04 us

profile of v4, /device:TPU:1, one launch (start us, length us, event | category | flops | bytes accessed | tf_op | source)
XLA Modules:
  0.0 70.0 jit_solution(15703637161137539505)
XLA Ops:
  0.6 64.6 %fused.1 = (f32[256,128]{1,0:T(8,128)}, f32[128,128]{1,0:T(8,128)}, f32[1,1]{1,0:T(1,128)}) custom-call(f32[256,128]{1,0:T(8,128)} %bitcast.10, f32[128,128]{1,0:T(8,128)} %bitcast.12, bf16[32,256,256]{2,1,0:T(8,128)(2,1)} %bitcast.8, s32[32,16,256]{2,1,0:T(8,128)} %bitcast.9, s32[32]{0:T(128)} %bitcast.14), custom_call_target="tpu_custom_call" | custom-call | tf_op jit(solution)/shard_map/fused/pallas_call | solution.py:372
  65.2 1.6 %copy.11 = f32[1,256,128]{2,1,0:T(8,128)} copy(f32[1,256,128]{2,1,0:T(8,128)} %bitcast.11) | data formatting | bytes 262144
  66.8 1.5 %copy.12 = f32[1,128,128]{2,1,0:T(8,128)} copy(f32[1,128,128]{2,1,0:T(8,128)} %bitcast.13) | data formatting | bytes 131072

commit v5 on v4

--- a/solution.py
+++ b/solution.py
@@ -71,7 +71,7 @@
 UNROLL = 4
 
 
-def fused_kernel(entries, fu_hbm, fv_hbm, vals_hbm, mask_hbm, ids_ref, nu_ref, nv_ref, loss_ref,
+def fused_kernel(entries, fu_hbm, fv_hbm, vals_hbm, mask_hbm, ids_ref, out_ref, loss_ref,
                  fu_ref, fv_ref, u, v, vals, mask, prev, chain, pu, pv, ls, pb, t, xb, w, w0, zb, yb, wl, wl0, lb, le, ln, lz, lx,
                  load_sems, send_sems, recv_sems):
     p = Place()
@@ -297,8 +297,8 @@
     for d in (-1, 1, 2):
         xin(2, d)
     squares = work(1, 1, squares)
+    s1(1, 0)
     squares = work(2, 0, squares)
-    s1(1, 0)
     s1(1, 1)
     xin(3, -1)
     xin(3, 1)
@@ -342,7 +342,7 @@
         net.recv(("l", l), wl0.at[l], p.dev(dl=l))
     grad = (mine + f(wl0.at[1])) + (f(wl0.at[2]) + f(wl0.at[3]))
     old = fv_ref[...]
-    nv_ref[...] = old - STEP * (grad + RIDGE * old)
+    out_ref[pl.ds(256, 128)] = old - STEP * (grad + RIDGE * old)
     shared(1, axes[1])
     loss_ref[0, 0] = jnp.sum(ln[2]) * (1.0 / entries)
     for j in (1, 2, 3):
@@ -350,7 +350,7 @@
             net.recv(("z", j, h), zb.at[j, cut(j, h)], p.dev(dz=DZ[j]))
     grad = (w0[...] + f(zb.at[1])) + (f(zb.at[2]) + f(zb.at[3]))
     old = fu_ref[...]
-    nu_ref[...] = old - STEP * (grad + RIDGE * old)
+    out_ref[pl.ds(0, 256)] = old - STEP * (grad + RIDGE * old)
     net.finish()
 
 
@@ -369,12 +369,11 @@
     def full(*shape):
         return pltpu.VMEM(shape, F32)
 
-    new_u, new_v, loss = pl.pallas_call(
+    out, loss = pl.pallas_call(
         lambda *refs: fused_kernel(entries, *refs),
-        out_shape=(jax.ShapeDtypeStruct((256, 128), F32), jax.ShapeDtypeStruct((128, 128), F32),
-                   jax.ShapeDtypeStruct((1, 1), F32)),
+        out_shape=(jax.ShapeDtypeStruct((384, 128), F32), jax.ShapeDtypeStruct((1, 1), F32)),
         in_specs=[far, far, far, far, near],
-        out_specs=(vmem(), vmem(), near),
+        out_specs=(vmem(), near),
         scratch_shapes=[
             full(256, 128),
             full(128, 128),
@@ -408,6 +407,22 @@
         compiler_params=pltpu.CompilerParams(collective_id=0, has_side_effects=True),
         name="fused",
     )(factor_u[0], factor_v[0], values[0, 0], mask_words[0, 0], tile_cols[0, 0])
+    def close(out_ref, u_hbm, v_hbm, sems):
+        one = pltpu.make_async_copy(out_ref.at[pl.ds(0, 256)], u_hbm, sems.at[0])
+        two = pltpu.make_async_copy(out_ref.at[pl.ds(256, 128)], v_hbm, sems.at[1])
+        one.start()
+        two.start()
+        one.wait()
+        two.wait()
+
+    new_u, new_v = pl.pallas_call(
+        close,
+        out_shape=(jax.ShapeDtypeStruct((256, 128), F32), jax.ShapeDtypeStruct((128, 128), F32)),
+        in_specs=[vmem()],
+        out_specs=(far, far),
+        scratch_shapes=[pltpu.SemaphoreType.DMA((2,))],
+        name="close",
+    )(out)
     return new_u[None], new_v[None], loss[0, 0]
 
 

time: 70.3 us -> 68 us (0.967)
  local copies, waits for them, and re-layouts: 3.04 us -> 0 us
  Pallas kernels: 64.6 us -> 65.5 us
    unnamed x2 -> x0, local copies, waits for them, and re-layouts: 3.04 us -> none
    pallas_call x0 -> x1, Pallas kernels: none -> 1.62 us  [per_device(): pl.pallas_call(close, out_shape=(jax.ShapeDtypeStruct((256, 128), F32), j...]
    pallas_call x1, Pallas kernels: 64.6 us -> 63.9 us  [per_device(): pl.pallas_call(lambda *refs: fused_kernel(entries, *refs), out_shape=(jax...]
where the time goes in v5:
time: 68 us; the launch traced here: 67.8 us
  Pallas kernels  65.5 us (96%)
  between operations  2.33 us (3%)
    pallas_call x1, Pallas kernels, per_device(): pl.pallas_call(lambda *refs: fused_kernel(entries, *refs), out_shape=(jax...  63.9 us
    pallas_call x1, Pallas kernels, per_device(): pl.pallas_call(close, out_shape=(jax.ShapeDtypeStruct((256, 128), F32), j...  1.62 us

profile of v5, /device:TPU:1, one launch (start us, length us, event | category | flops | bytes accessed | tf_op | source)
XLA Modules:
  0.0 67.8 jit_solution(7599827729784963351)
XLA Ops:
  0.6 63.9 %fused.1 = (f32[384,128]{1,0:T(8,128)}, f32[1,1]{1,0:T(1,128)}) custom-call(f32[256,128]{1,0:T(8,128)} %bitcast.10, f32[128,128]{1,0:T(8,128)} %bitcast.11, bf16[32,256,256]{2,1,0:T(8,128)(2,1)} %bitcast.8, s32[32,16,256]{2,1,0:T(8,128)} %bitcast.9, s32[32]{0:T(128)} %bitcast.12), custom_call_target="tpu_custom_call" | custom-call | tf_op jit(solution)/shard_map/fused/pallas_call | solution.py:372
  64.5 1.6 %close.1 = (f32[256,128]{1,0:T(8,128)}, f32[128,128]{1,0:T(8,128)}) custom-call(f32[384,128]{1,0:T(8,128)} %get-tuple-element.7.out_ref), custom_call_target="tpu_custom_call" | custom-call | tf_op jit(solution)/shard_map/close/pallas_call | solution.py:418
